TPU v7x, 32 devices: a whole 2x2x4 slice. The times are simulated.
32 devices in a mesh: dp: 2 (over x), tp: 16 (over z, y, core).
Axes of the slice: x: 2, y: 2, z: 4, core: 2. Of those that a mesh axis runs over, the one named last changes fastest.
Arguments:
- x_norm: bfloat16 [8192, 2048], P(('dp', 'tp')), parts along dimension 0
- grad_y: bfloat16 [8192, 2048], P(('dp', 'tp')), parts along dimension 0
- u_gate: bfloat16 [8192, 11008], P('dp', 'tp'), parts along dimension 0
- u_up: bfloat16 [8192, 11008], P('dp', 'tp'), parts along dimension 0
- w_gate: bfloat16 [2048, 11008], P(None, 'tp')
- w_up: bfloat16 [2048, 11008], P(None, 'tp')
- w_down: bfloat16 [11008, 2048], P('tp')
- x_in: bfloat16 [8192, 2048], P(('dp', 'tp')), parts along dimension 0
- gamma: bfloat16 [2048], replicated
- grad_res: bfloat16 [8192, 2048], P(('dp', 'tp')), parts along dimension 0
- attn_out: bfloat16 [8192, 2048], P('dp', 'tp'), parts along dimension 0
- w_out: bfloat16 [2048, 2048], P('tp')
Outputs:
- output 1: bfloat16 [8192, 2048], P(('dp', 'tp')), parts along dimension 0
- output 2: bfloat16 [8192, 2048], P('dp', 'tp'), parts along dimension 0
- output 3: float32 [4096, 11008], P('dp', 'tp'), parts along dimension 0
- output 4: float32 [4096, 11008], P('dp', 'tp'), parts along dimension 0
- output 5: float32 [22016, 2048], P(('dp', 'tp')), parts along dimension 0
- output 6: float32 [4096, 2048], P(('dp', 'tp')), parts along dimension 0
There are 2 independent parts. A program takes and returns all parts, laid end to end along the dimension named above; an argument that names none is the same for every part.
All inputs are finite; a program needn't handle non-finite values.
Results may differ from a plain program's by a relative error of at most 0.0148682.
Values are sent between devices in bfloat16 or wider.
A program may use at most 1 GiB of HBM per device.

v0:
```python
import jax
import jax.numpy as jnp
from jax import lax
from jax.sharding import PartitionSpec as P

NORM_EPS = 1e-5
CONTRACT_ROWS = (((0,), (0,)), ((), ()))
CONTRACT_COLS = (((1,), (1,)), ((), ()))


def rms_backward(grad_x, x_in, gamma, grad_res):
    xin_f = x_in.astype(jnp.float32)
    inv_rms = lax.rsqrt(jnp.mean(xin_f * xin_f, axis=-1, keepdims=True) + NORM_EPS)
    scaled = grad_x.astype(jnp.float32) * gamma.astype(jnp.float32)
    proj_mean = jnp.mean(scaled * xin_f, axis=-1, keepdims=True)
    return (grad_res.astype(jnp.float32)
            + inv_rms * (scaled - xin_f * (inv_rms * inv_rms) * proj_mean)).astype(jnp.bfloat16)


def solution(mesh):
    token_spec = P(("dp", "tp"), None)
    split_cols = P("dp", "tp")
    weight_cols = P(None, "tp")
    weight_rows = P("tp", None)

    def local_backward(x_norm, grad_y, u_gate, u_up, w_gate, w_up, w_down, x_in, gamma, grad_res, attn_out, w_out):
        x_full = lax.all_gather(x_norm, "tp", axis=0, tiled=True)
        gy_full = lax.all_gather(grad_y, "tp", axis=0, tiled=True)
        gate_f = u_gate.astype(jnp.float32)
        up_f = u_up.astype(jnp.float32)
        sig_gate = jax.nn.sigmoid(gate_f)
        act_gate = gate_f * sig_gate
        silu_grad = sig_gate * (1.0 + gate_f * (1.0 - sig_gate))
        hidden_z = (act_gate * up_f).astype(jnp.bfloat16)
        gw_down = lax.dot_general(hidden_z, gy_full, CONTRACT_ROWS, preferred_element_type=jnp.float32)
        grad_h = lax.dot_general(gy_full, w_down, CONTRACT_COLS, preferred_element_type=jnp.float32)
        grad_up = (grad_h * act_gate).astype(jnp.bfloat16)
        grad_gate = (grad_h * up_f * silu_grad).astype(jnp.bfloat16)
        part_x = (lax.dot_general(grad_gate, w_gate, CONTRACT_COLS, preferred_element_type=jnp.float32)
                  + lax.dot_general(grad_up, w_up, CONTRACT_COLS, preferred_element_type=jnp.float32))
        grad_x = lax.psum_scatter(part_x.astype(jnp.bfloat16), "tp", scatter_dimension=0, tiled=True)
        gw_gate = lax.dot_general(x_full, grad_gate, CONTRACT_ROWS, preferred_element_type=jnp.float32)
        gw_up = lax.dot_general(x_full, grad_up, CONTRACT_ROWS, preferred_element_type=jnp.float32)
        grad_sum = rms_backward(grad_x, x_in, gamma, grad_res)
        gs_full = lax.all_gather(grad_sum, "tp", axis=0, tiled=True)
        grad_attn = lax.dot_general(gs_full, w_out, CONTRACT_COLS, preferred_element_type=jnp.float32).astype(jnp.bfloat16)
        gw_out = lax.dot_general(attn_out, gs_full, CONTRACT_ROWS, preferred_element_type=jnp.float32)
        return grad_sum, grad_attn, gw_gate, gw_up, gw_down, gw_out

    return jax.shard_map(
        local_backward,
        mesh=mesh,
        in_specs=(token_spec, token_spec, split_cols, split_cols, weight_cols, weight_cols, weight_rows,
                  token_spec, P(None), token_spec, split_cols, weight_rows),
        out_specs=(token_spec, split_cols, split_cols, split_cols, token_spec, token_spec),
        check_vma=False,
    )
```

profile of v0, /device:TPU:0, one launch (start us, length us, event | category | flops | bytes accessed | tf_op | source)
XLA Modules:
  0.0 665.1 jit_solution(10231342495478905714)
XLA Ops:
  7.2 0.0 copy-start
  7.2 0.0 all-gather.4.cloned.1.call-start
  7.2 0.7 all-gather.4.cloned.1.call-update
  7.9 0.0 reduce-scatter.2.cloned.1.call-start
  8.0 130.7 %all-gather.4.cloned.1.call-done = bf16[4096,2048]{1,0:T(8,128)(2,1)} async-done(((bf16[256,2048]{1,0:T(8,128)(2,1)}), bf16[4096,2048]{1,0:T(8,128)(2,1)}) %all-gather.4.cloned.1.call-update) | async-done | bytes 16777232 | tf_op jit(solution)/shard_map/all_gather | solution.py:28
  138.7 24.8 %fusion.1 = (bf16[4096,688]{0,1:T(8,128)(2,1)}, f32[4096,688]{0,1:T(8,128)}) fusion(bf16[4096,688]{0,1:T(8,128)(2,1)} %param.15, bf16[4096,688]{0,1:T(8,128)(2,1)} %param.14, bf16[4096,2048]{1,0:T(8,128)(2,1)} %all-gather.4.cloned.1.call-done, bf16[688,2048]{1,0:T(8,128)(2,1)} %param.18), kind=kOutput, calls=%fused_computation.7 | convolution fusion | flops 11576541184 | bytes 47775744 | tf_op jit(solution)/shard_map/dot_general | solution.py:36
  163.5 0.0 copy-done
  163.5 20.0 %fusion.19 = f32[4096,2048]{1,0:T(8,128)} fusion(bf16[4096,688]{0,1:T(8,128)(2,1)} %get-tuple-element.16, bf16[2048,688]{0,1:T(8,128)(2,1)S(1)} %copy-done), kind=kOutput, calls=%fused_computation.35 | convolution fusion | flops 11542724608 | bytes 42008576 | tf_op jit(solution)/shard_map/dot_general | solution.py:39
  183.5 0.0 copy-done.5
  183.6 25.1 %add_convert_fusion = bf16[4096,2048]{1,0:T(8,128)(2,1)} fusion(f32[4096,2048]{1,0:T(8,128)} %fusion.19, bf16[2048,688]{0,1:T(8,128)(2,1)} %param.17, f32[4096,688]{0,1:T(8,128)} %get-tuple-element.17, bf16[4096,688]{0,1:T(8,128)(2,1)S(1)} %copy-done.5), kind=kOutput, calls=%fused_computation | convolution fusion | flops 11579228160 | bytes 70057984 | tf_op jit(solution)/shard_map/dot_general | solution.py:40
  208.7 0.0 reduce-scatter.2.cloned.1.call-update
  208.7 0.0 all-gather.8.cloned.1.call-start
  208.7 0.7 all-gather.8.cloned.1.call-update
  209.4 0.0 all-gather.6.cloned.1.call-start
  209.5 0.0 copy-done.4
  209.5 173.6 %reduce-scatter.2.cloned.1.call-done = bf16[256,2048]{1,0:T(8,128)(2,1)} async-done(((bf16[4096,2048]{1,0:T(8,128)(2,1)}), bf16[256,2048]{1,0:T(8,128)(2,1)}) %reduce-scatter.2.cloned.1.call-update) | async-done | bytes 1048592 | tf_op jit(solution)/shard_map/reduce_scatter | solution.py:41
  383.1 0.0 copy-done.2
  383.1 1.8 fusion.10
  384.9 0.0 copy-done.3
  384.9 3.1 fusion.15
  387.9 0.0 all-gather.6.cloned.1.call-update
  388.0 122.6 %all-gather.8.cloned.1.call-done = bf16[4096,2048]{1,0:T(8,128)(2,1)} async-done(((bf16[256,2048]{1,0:T(8,128)(2,1)}), bf16[4096,2048]{1,0:T(8,128)(2,1)}) %all-gather.8.cloned.1.call-update) | async-done | bytes 16777232 | tf_op jit(solution)/shard_map/all_gather | solution.py:27
  510.5 18.6 %convolution_bitcast_fusion.1 = f32[2048,688]{0,1:T(8,128)} fusion(bf16[4096,688]{0,1:T(8,128)(2,1)} %get-tuple-element.16, bf16[4096,2048]{1,0:T(8,128)(2,1)} %all-gather.8.cloned.1.call-done), kind=kOutput, calls=%fused_computation.18 | convolution fusion | flops 11542724608 | bytes 28049408 | tf_op jit(solution)/shard_map/dot_general | solution.py:42
  529.2 21.8 %fusion.8 = f32[688,2048]{1,0:T(8,128)} fusion(bf16[4096,2048]{1,0:T(8,128)(2,1)} %all-gather.4.cloned.1.call-done, bf16[4096,688]{0,1:T(8,128)(2,1)} %param.15, bf16[4096,688]{0,1:T(8,128)(2,1)} %param.14), kind=kOutput, calls=%fused_computation.15 | convolution fusion | flops 11565268992 | bytes 33685504 | tf_op jit(solution)/shard_map/dot_general | solution.py:35
  551.0 0.0 slice-done
  551.0 0.0 slice-done.1
  551.0 0.0 copy-start.6
  551.0 21.1 %convolution_bitcast_fusion = f32[2048,688]{0,1:T(8,128)} fusion(bf16[4096,2048]{1,0:T(8,128)(2,1)} %all-gather.8.cloned.1.call-done, f32[4096,688]{0,1:T(8,128)} %get-tuple-element.17, bf16[4096,688]{0,1:T(8,128)(2,1)S(1)} %bitcast.20), kind=kOutput, calls=%fused_computation.17 | convolution fusion | flops 11562450944 | bytes 39321600 | tf_op jit(solution)/shard_map/dot_general | solution.py:43
  572.1 65.5 %all-gather.6.cloned.1.call-done = bf16[4096,2048]{1,0:T(8,128)(2,1)} async-done(((bf16[256,2048]{1,0:T(8,128)(2,1)}), bf16[4096,2048]{1,0:T(8,128)(2,1)}) %all-gather.6.cloned.1.call-update) | async-done | bytes 16777232 | tf_op jit(solution)/shard_map/all_gather | solution.py:45
  637.6 9.1 %convolution_bitcast_fusion.2 = f32[128,2048]{0,1:T(8,128)} fusion(bf16[4096,2048]{1,0:T(8,128)(2,1)} %all-gather.6.cloned.1.call-done, bf16[4096,128]{1,0:T(8,128)(2,1)S(1)} %copy-done.6), kind=kOutput, calls=%fused_computation.22 | convolution fusion | flops 2147483648 | bytes 18874368 | tf_op jit(solution)/shard_map/dot_general | solution.py:47
  646.7 2.7 copy.18
  649.4 9.2 %convolution_convert_fusion = bf16[4096,128]{1,0:T(8,128)(2,1)} fusion(bf16[4096,2048]{1,0:T(8,128)(2,1)} %all-gather.6.cloned.1.call-done, bf16[128,2048]{1,0:T(8,128)(2,1)S(1)} %copy-done.7), kind=kOutput, calls=%fused_computation.16 | convolution fusion | flops 2148007936 | bytes 18350080 | tf_op jit(solution)/shard_map/dot_general | solution.py:46
  (15 shorter events, 0.0 us)
Async XLA Ops:
  7.2 156.3 %copy-start = (bf16[2048,688]{0,1:T(8,128)(2,1)S(1)}, bf16[2048,688]{0,1:T(8,128)(2,1)}, u32[]{:S(2)}) copy-start(bf16[2048,688]{0,1:T(8,128)(2,1)} %param.16) | copy-start | bytes 8454148
  7.2 131.5 %all-gather.4.cloned.1.call-start = ((), (), s32[]{:S(2)}) async-start(), calls=%async_computation.1 | async-start | bytes 17825792 | tf_op jit(solution)/shard_map/all_gather | solution.py:28
  7.9 375.1 %reduce-scatter.2.cloned.1.call-start = ((), (), s32[]{:S(2)}) async-start(), calls=%async_computation.2 | async-start | bytes 17825792 | tf_op jit(solution)/shard_map/reduce_scatter | solution.py:41
  163.5 20.0 %copy-start.5 = (bf16[4096,688]{0,1:T(8,128)(2,1)S(1)}, bf16[4096,688]{0,1:T(8,128)(2,1)}, u32[]{:S(2)}) copy-start(bf16[4096,688]{0,1:T(8,128)(2,1)} %param.14) | copy-start | bytes 16908292
  208.6 0.8 copy-start.4
  208.6 174.4 %copy-start.2 = (bf16[256,2048]{1,0:T(8,128)(2,1)S(1)}, bf16[256,2048]{1,0:T(8,128)(2,1)}, u32[]{:S(2)}) copy-start(bf16[256,2048]{1,0:T(8,128)(2,1)} %param.19) | copy-start | bytes 3145732
  208.6 176.2 %copy-start.3 = (bf16[256,2048]{1,0:T(8,128)(2,1)S(1)}, bf16[256,2048]{1,0:T(8,128)(2,1)}, u32[]{:S(2)}) copy-start(bf16[256,2048]{1,0:T(8,128)(2,1)} %param.21) | copy-start | bytes 3145732
  208.7 301.9 %all-gather.8.cloned.1.call-start = ((), (), s32[]{:S(2)}) async-start(), calls=%async_computation.4 | async-start | bytes 17825792 | tf_op jit(solution)/shard_map/all_gather | solution.py:27
  209.4 428.2 %all-gather.6.cloned.1.call-start = ((), (), s32[]{:S(2)}) async-start(), calls=%async_computation.3 | async-start | bytes 17825792 | tf_op jit(solution)/shard_map/all_gather | solution.py:45
  510.5 40.4 %slice-start = ((s8[5636096]{0:T(1024)(128)(4,1)}), s8[4194304]{0:T(1024)(128)(4,1)S(1)}, s32[]{:S(2)}) async-start(s8[5636096]{0:T(1024)(128)(4,1)} %bitcast.19), calls=%async_computation.5 | async-start | bytes 8388608
  529.2 21.8 %slice-start.1 = ((s8[5636096]{0:T(1024)(128)(4,1)}), s8[1441792]{0:T(1024)(128)(4,1)S(1)}, s32[]{:S(2)}) async-start(s8[5636096]{0:T(1024)(128)(4,1)} %bitcast.19), calls=%async_computation.6 | async-start | bytes 2883584
  551.0 86.6 %copy-start.6 = (bf16[4096,128]{1,0:T(8,128)(2,1)S(1)}, bf16[4096,128]{1,0:T(8,128)(2,1)}, u32[]{:S(2)}) copy-start(bf16[4096,128]{1,0:T(8,128)(2,1)} %param.22) | copy-start | bytes 3145732
  572.1 77.3 %copy-start.7 = (bf16[128,2048]{1,0:T(8,128)(2,1)S(1)}, bf16[128,2048]{1,0:T(8,128)(2,1)}, u32[]{:S(2)}) copy-start(bf16[128,2048]{1,0:T(8,128)(2,1)} %param.23) | copy-start | bytes 1572868
  646.7 11.9 %copy-start.1 = (bf16[2048,688]{0,1:T(8,128)(2,1)S(1)}, bf16[2048,688]{0,1:T(8,128)(2,1)}, u32[]{:S(2)}) copy-start(bf16[2048,688]{0,1:T(8,128)(2,1)} %param.16) | copy-start | bytes 8454148
Sparse Core Ops, SparseCore 0:
  10.2 128.4 all-gather.3
  208.8 174.2 reduce-scatter.1
  385.2 125.2 all-gather.7
  513.1 124.3 all-gather.5
where the time goes:
time: 665 us
  waiting for transfers between devices  494 us (74%)
  matrix products  150 us (23%)
  between operations  13.8 us (2%)
    reduce_scatter x1, waiting for transfers between devices, local_backward(): lax.psum_scatter(part_x.astype(jnp.bfloat16), 'tp', scatter_dimension=0,...  174 us
    all_gather x1, waiting for transfers between devices, local_backward(): gy_full = lax.all_gather(grad_y, 'tp', axis=0, tiled=True)  131 us
    all_gather x1, waiting for transfers between devices, local_backward(): x_full = lax.all_gather(x_norm, 'tp', axis=0, tiled=True)  123 us
    all_gather x1, waiting for transfers between devices, local_backward(): gs_full = lax.all_gather(grad_sum, 'tp', axis=0, tiled=True)  65.5 us
    dot_general x1, matrix products, local_backward(): lax.dot_general(grad_up, w_up, CONTRACT_COLS, preferred_element_type=jnp....  25.1 us
    dot_general x1, matrix products, local_backward(): lax.dot_general(gy_full, w_down, CONTRACT_COLS, preferred_element_type=jn...  24.8 us
    dot_general x1, matrix products, local_backward(): lax.dot_general(hidden_z, gy_full, CONTRACT_ROWS, preferred_element_type=...  21.8 us
    dot_general x1, matrix products, local_backward(): lax.dot_general(x_full, grad_up, CONTRACT_ROWS, preferred_element_type=jn...  21.1 us
  transfers between devices with their start and end apart: 4, of which 4 were waited for; matrix products, arithmetic and copies ran while one was open for 10% of the time, Pallas kernels for 0%

commit v1 on v0

v1 whole, which is shorter than its diff:
```python
import jax
import jax.numpy as jnp
from jax import lax
from jax.experimental import pallas as pl
from jax.experimental.pallas import tpu as pltpu
from jax.sharding import PartitionSpec as P

NORM_EPS = 1e-5
MESH = pl.DeviceIdType.MESH
BF16 = jnp.bfloat16
F32 = jnp.float32

CHIPS = 8
QUARTER = 128
HALF = 64
ROWS = 4 * QUARTER
LAST = CHIPS - 1


def dot_cols(a, b):
    return lax.dot_general(a, b, (((1,), (1,)), ((), ())), preferred_element_type=F32)


def dot_plain(a, b):
    return lax.dot_general(a, b, (((1,), (0,)), ((), ())), preferred_element_type=F32)


def kernel(x, gy, ug, uu, wg, wu, wd, xin, gamma, gres, att, wo,
           out_ds, out_do, out_wg, out_wu, out_wd, out_wo, gy_all, x_all, ds_all,
           wg_v, wu_v, wd_v, acc_g, acc_u, acc_d,
           gy_b, x_b, ug_b, uu_b, z_b, dg_b, du_b, zt_b, xt_b,
           p_own, p_send, p_recv, rs_send, rs_recv, own_sum,
           att_v, wo_v, do_v, acc_o,
           gy_ss, gy_rs, gy_ps, gy_pr, x_ss, x_rs, x_ps, x_pr,
           ds_ss, ds_rs, ds_ps, ds_pr, ps_sem, pr_sem, rss_sem, rsr_sem,
           w_sem, gy_sem, x_sem, ug_sem, uu_sem, o_sem):
    hidden = gy.shape[1]
    t = lax.axis_index("tp")
    core = t % 2
    y = (t // 2) % 2
    z = t // 4
    pos = z + y * (7 - 2 * z)

    def device(chip, c):
        upper = chip // 4
        return 4 * (chip + upper * (7 - 2 * chip)) + 2 * upper + c

    right = device((pos + 1) % CHIPS, core)
    left = device((pos + LAST) % CHIPS, core)
    onward = (right, left)
    twin = t + 1 - 2 * core

    barrier = pltpu.get_barrier_semaphore()
    for other in (right, left, twin):
        pl.semaphore_signal(barrier, inc=1, device_id={"tp": other}, device_id_type=MESH)
    pl.semaphore_wait(barrier, 3)

    def row(s, d, c):
        source = (pos + (CHIPS - s if d == 0 else s)) % CHIPS
        return pl.multiple_of(device(source, c) * 2 * QUARTER + d * QUARTER, QUARTER)

    def remote(src, dst, send, recv, to):
        return pltpu.make_async_remote_copy(src_ref=src, dst_ref=dst, send_sem=send, recv_sem=recv,
                                            device_id={"tp": to}, device_id_type=MESH)

    def pass_on(full, ss, rs, s, d, src=None):
        rows = pl.ds(row(s - 1, d, core), QUARTER)
        return remote(full.at[rows, :] if src is None else src, full.at[rows, :],
                      ss.at[s, d], rs.at[s, d], onward[d])

    def arriving(full, ss, rs, s, d):
        rows = pl.ds(row(s, d, core), QUARTER)
        return remote(full.at[rows, :], full.at[rows, :], ss.at[s, d], rs.at[s, d], onward[d])

    def to_twin(full, ss, rs, s, d, src=None):
        rows = pl.ds(row(s, d, core), QUARTER)
        return remote(full.at[rows, :] if src is None else src, full.at[rows, :],
                      ss.at[s, d], rs.at[s, d], twin)

    def from_twin(full, ss, rs, s, d):
        rows = pl.ds(row(s, d, 1 - core), QUARTER)
        return remote(full.at[rows, :], full.at[rows, :], ss.at[s, d], rs.at[s, d], twin)

    streams = ((gy, gy_all, gy_ss, gy_rs, gy_ps, gy_pr), (x, x_all, x_ss, x_rs, x_ps, x_pr))
    for own, full, ss, rs, ps, pr in streams:
        for d in (0, 1):
            mine = own.at[pl.ds(d * QUARTER, QUARTER), :]
            pass_on(full, ss, rs, 1, d, mine).start()
            to_twin(full, ps, pr, 0, d, mine).start()

    def load(src, dst, i):
        return pltpu.make_async_copy(src, dst, w_sem.at[i])

    loads = [load(a, b, i) for i, (a, b) in enumerate(
        ((wd, wd_v), (wg, wg_v), (wu, wu_v), (att, att_v), (wo, wo_v)))]
    for copy in loads:
        copy.start()

    def load_u(s):
        copies = []
        for d in (0, 1):
            for k in (0, 1):
                c = core if k == 0 else 1 - core
                rows = pl.ds(row(s, d, c), QUARTER)
                at = pl.ds((2 * k + d) * QUARTER, QUARTER)
                copies.append(pltpu.make_async_copy(ug.at[rows, :], ug_b.at[at, :], ug_sem.at[2 * k + d]))
                copies.append(pltpu.make_async_copy(uu.at[rows, :], uu_b.at[at, :], uu_sem.at[2 * k + d]))
        return copies

    for copy in load_u(0):
        copy.start()

    acc_g[...] = jnp.zeros_like(acc_g)
    acc_u[...] = jnp.zeros_like(acc_u)
    acc_d[...] = jnp.zeros_like(acc_d)
    acc_o[...] = jnp.zeros_like(acc_o)
    rs_recv[1] = jnp.zeros_like(rs_recv[1])

    def block_load(own, full, buf, sem, s, d, k):
        c = core if k == 0 else 1 - core
        at = pl.ds((2 * k + d) * QUARTER, QUARTER)
        if own is not None:
            return pltpu.make_async_copy(own.at[pl.ds(d * QUARTER, QUARTER), :], buf.at[at, :], sem.at[2 * k + d])
        return pltpu.make_async_copy(full.at[pl.ds(row(s, d, c), QUARTER), :], buf.at[at, :], sem.at[2 * k + d])

    def receive(stream, buf, sem, s):
        own, full, ss, rs, ps, pr = stream

        @pl.when(s > 0)
        def _():
            for d in (0, 1):
                arriving(full, ss, rs, s, d).wait_recv()

                @pl.when(s < LAST)
                def _():
                    pass_on(full, ss, rs, s + 1, d).start()
                to_twin(full, ps, pr, s, d).start()
            for d in (0, 1):
                block_load(None, full, buf, sem, s, d, 0).start()

        @pl.when(s == 0)
        def _():
            for d in (0, 1):
                block_load(own, full, buf, sem, s, d, 0).start()
        for d in (0, 1):
            from_twin(full, ps, pr, s, d).wait_recv()
            block_load(None, full, buf, sem, s, d, 1).start()

    def landed(full, buf, sem, s):
        for k in (0, 1):
            for d in (0, 1):
                block_load(None, full, buf, sem, s, d, k).wait()

    def swap(s):
        return remote(p_send, p_recv.at[s % 2], ps_sem, pr_sem.at[s % 2], twin)

    def sum_on(s, d):
        return remote(rs_send.at[s % 2, d], rs_recv.at[(s + 1) % 3, d],
                      rss_sem.at[s % 2, d], rsr_sem.at[(s + 1) % 3, d], onward[d])

    def sum_in(s, d):
        return remote(rs_send.at[0, d], rs_recv.at[s % 3, d],
                      rss_sem.at[0, d], rsr_sem.at[s % 3, d], onward[d])

    def step(s, carry):
        receive(streams[0], gy_b, gy_sem, s)
        for copy in load_u(s):
            copy.wait()

        @pl.when(s == 0)
        def _():
            for copy in loads:
                copy.wait()
        landed(gy_all, gy_b, gy_sem, s)

        def hidden_tile(i, carry):
            at = pl.ds(pl.multiple_of(i * 128, 128), 128)
            grad_h = dot_cols(gy_b[at, :], wd_v[...])
            gate = ug_b[at, :].astype(F32)
            up = uu_b[at, :].astype(F32)
            sig = jax.nn.sigmoid(gate)
            act = gate * sig
            z_b[at, :] = (act * up).astype(BF16)
            du_b[at, :] = (grad_h * act).astype(BF16)
            dg_b[at, :] = (grad_h * up * (sig * (1.0 + gate * (1.0 - sig)))).astype(BF16)
            return carry
        lax.fori_loop(0, ROWS // 128, hidden_tile, 0)

        @pl.when(s < LAST)
        def _():
            for copy in load_u(s + 1):
                copy.start()

        @pl.when(s > 0)
        def _():
            swap(s - 1).wait_send()

        def part_tile(j, carry):
            at = pl.ds(pl.multiple_of(j * 512, 512), 512)
            part = dot_cols(dg_b[...], wg_v[at, :]) + dot_cols(du_b[...], wu_v[at, :])
            p_own[:, at] = part[:2 * QUARTER]
            p_send[:, at] = part[2 * QUARTER:].astype(BF16)
            return carry
        lax.fori_loop(0, hidden // 512, part_tile, 0)
        swap(s).start()

        receive(streams[1], x_b, x_sem, s)

        def zt_tile(i, carry):
            at = pl.ds(pl.multiple_of(i * 128, 128), 128)
            zt_b[:, at] = z_b[at, :].T
            return carry
        lax.fori_loop(0, ROWS // 128, zt_tile, 0)

        swap(s).wait_recv()

        @pl.when(s == 0)
        def _():
            def tile(i, carry):
                at = pl.ds(pl.multiple_of(i * 32, 32), 32)
                own_sum[at, :] = p_own[at, :] + p_recv[0, at, :].astype(F32)
                return carry
            lax.fori_loop(0, 2 * QUARTER // 32, tile, 0)

        @pl.when(s > 0)
        def _():
            for d in (0, 1):
                @pl.when(s > 1)
                def _():
                    sum_in(s, d).wait_recv()

                @pl.when(s > 2)
                def _():
                    sum_on(s - 2, d).wait_send()

                def tile(i, carry):
                    at = pl.ds(pl.multiple_of(i * 32, 32), 32)
                    here = pl.ds(pl.multiple_of(d * QUARTER + i * 32, 32), 32)
                    total = (p_own[here, :] + p_recv[s % 2, here, :].astype(F32)
                             + rs_recv[s % 3, d, at, :].astype(F32))
                    rs_send[s % 2, d, at, :] = total.astype(BF16)
                    return carry
                lax.fori_loop(0, QUARTER // 32, tile, 0)
                sum_on(s, d).start()

        def down_tile(j, carry):
            at = pl.ds(pl.multiple_of(j * 512, 512), 512)
            acc_d[:, at] += dot_plain(zt_b[...], gy_b[:, at])
            return carry
        lax.fori_loop(0, hidden // 512, down_tile, 0)

        landed(x_all, x_b, x_sem, s)

        def xt_tile(i, carry):
            at = pl.ds(pl.multiple_of(i * 128, 128), 128)
            xt_b[at, :] = x_b[:, at].T
            return carry
        lax.fori_loop(0, hidden // 128, xt_tile, 0)

        def up_tile(i, carry):
            at = pl.ds(pl.multiple_of(i * 512, 512), 512)
            acc_g[at, :] += dot_plain(xt_b[at, :], dg_b[...])
            acc_u[at, :] += dot_plain(xt_b[at, :], du_b[...])
            return carry
        lax.fori_loop(0, hidden // 512, up_tile, 0)
        return carry

    lax.fori_loop(0, CHIPS, step, 0)

    stores = [pltpu.make_async_copy(a, b, o_sem.at[i]) for i, (a, b) in enumerate(
        ((acc_g, out_wg), (acc_u, out_wu), (acc_d, out_wd)))]
    for copy in stores:
        copy.start()

    norm_loads = [pltpu.make_async_copy(src, x_b.at[pl.ds(k * 2 * QUARTER, 2 * QUARTER), :], x_sem.at[k])
                  for k, src in enumerate((xin, gres))]
    for copy in norm_loads:
        copy.start()
    for copy in norm_loads:
        copy.wait()
    swap(LAST).wait_send()

    def ds_next(s, d, h, src=None):
        rows = pl.ds(pl.multiple_of(row(s - 1, d, core) + h * HALF, HALF), HALF)
        return remote(ds_all.at[rows, :] if src is None else src, ds_all.at[rows, :],
                      ds_ss.at[s, 2 * d + h], ds_rs.at[s, 2 * d + h], onward[d])

    def ds_here(s, d, h):
        rows = pl.ds(pl.multiple_of(row(s, d, core) + h * HALF, HALF), HALF)
        return remote(ds_all.at[rows, :], ds_all.at[rows, :],
                      ds_ss.at[s, 2 * d + h], ds_rs.at[s, 2 * d + h], onward[d])

    def ds_twin(s, d, h, src=None):
        rows = pl.ds(pl.multiple_of(row(s, d, core) + h * HALF, HALF), HALF)
        return remote(ds_all.at[rows, :] if src is None else src, ds_all.at[rows, :],
                      ds_ps.at[s, 2 * d + h], ds_pr.at[s, 2 * d + h], twin)

    def ds_from_twin(s, d, h):
        rows = pl.ds(pl.multiple_of(row(s, d, 1 - core) + h * HALF, HALF), HALF)
        return remote(ds_all.at[rows, :], ds_all.at[rows, :],
                      ds_ps.at[s, 2 * d + h], ds_pr.at[s, 2 * d + h], twin)

    gain = gamma[...].astype(F32)
    for d in (0, 1):
        sum_in(CHIPS, d).wait_recv()
    for h in (0, 1):
        for d in (0, 1):
            def norm_tile(i, carry):
                at = pl.ds(pl.multiple_of(h * HALF + i * 16, 16), 16)
                here = pl.ds(pl.multiple_of(d * QUARTER + h * HALF + i * 16, 16), 16)
                skip = pl.ds(pl.multiple_of(2 * QUARTER + d * QUARTER + h * HALF + i * 16, 16), 16)
                grad_x = (own_sum[here, :] + rs_recv[CHIPS % 3, d, at, :].astype(F32)).astype(BF16).astype(F32)
                xin_f = x_b[here, :].astype(F32)
                inv_rms = lax.rsqrt(jnp.mean(xin_f * xin_f, axis=-1, keepdims=True) + NORM_EPS)
                scaled = grad_x * gain
                proj = jnp.mean(scaled * xin_f, axis=-1, keepdims=True)
                grad_s = (x_b[skip, :].astype(F32)
                          + inv_rms * (scaled - xin_f * (inv_rms * inv_rms) * proj)).astype(BF16)
                p_send[here, :] = grad_s
                gy_b[here, :] = grad_s
                return carry
            lax.fori_loop(0, HALF // 16, norm_tile, 0)
            mine = p_send.at[pl.ds(d * QUARTER + h * HALF, HALF), :]
            ds_next(1, d, h, mine).start()
            ds_twin(0, d, h, mine).start()
    store_ds = pltpu.make_async_copy(p_send, out_ds, o_sem.at[3])
    store_ds.start()

    def project(s):
        for d in (0, 1):
            for h in (0, 1):
                ds_from_twin(s, d, h).wait_recv()
            block_load(None, ds_all, gy_b, gy_sem, s, d, 1).start()
        for d in (0, 1):
            block_load(None, ds_all, gy_b, gy_sem, s, d, 1).wait()
        for k in (0, 1):
            for d in (0, 1):
                c = core if k == 0 else 1 - core
                rows = pl.ds(row(s, d, c), QUARTER)
                at = pl.ds((2 * k + d) * QUARTER, QUARTER)
                zt_b[pl.ds(0, QUARTER), at] = att_v[rows, :].T
        grad_o = dot_cols(gy_b[...], wo_v[...]).astype(BF16)
        for k in (0, 1):
            for d in (0, 1):
                c = core if k == 0 else 1 - core
                do_v[pl.ds(row(s, d, c), QUARTER), :] = grad_o[(2 * k + d) * QUARTER:(2 * k + d + 1) * QUARTER]
        for j in range(0, hidden, 512):
            acc_o[:, j:j + 512] += dot_plain(zt_b[pl.ds(0, QUARTER), :], gy_b[:, j:j + 512])

    def ds_relay(s, h):
        for d in (0, 1):
            ds_here(s, d, h).wait_recv()

            @pl.when(s < LAST)
            def _():
                ds_next(s + 1, d, h).start()
            ds_twin(s, d, h).start()

    def ds_step(s, carry):
        ds_relay(s, 0)
        project(s - 1)
        ds_relay(s, 1)
        for d in (0, 1):
            block_load(None, ds_all, gy_b, gy_sem, s, d, 0).start()
        for d in (0, 1):
            block_load(None, ds_all, gy_b, gy_sem, s, d, 0).wait()
        return carry

    lax.fori_loop(1, CHIPS, ds_step, 0)
    project(LAST)

    last = [pltpu.make_async_copy(do_v, out_do, o_sem.at[4]), pltpu.make_async_copy(acc_o, out_wo, o_sem.at[5])]
    for copy in last:
        copy.start()

    def drain(s, carry):
        for d in (0, 1):
            to_twin(gy_all, gy_ps, gy_pr, s, d).wait_send()
            to_twin(x_all, x_ps, x_pr, s, d).wait_send()
            for h in (0, 1):
                ds_twin(s, d, h).wait_send()

            @pl.when(s > 0)
            def _():
                arriving(gy_all, gy_ss, gy_rs, s, d).wait_send()
                arriving(x_all, x_ss, x_rs, s, d).wait_send()
                for h in (0, 1):
                    ds_here(s, d, h).wait_send()
        return carry
    lax.fori_loop(0, CHIPS, drain, 0)
    for d in (0, 1):
        sum_on(LAST - 1, d).wait_send()
        sum_on(LAST, d).wait_send()
    for copy in stores + [store_ds] + last:
        copy.wait()


def solution(mesh):
    token_spec = P(("dp", "tp"), None)
    split_cols = P("dp", "tp")
    weight_cols = P(None, "tp")
    weight_rows = P("tp", None)

    def local_backward(x_norm, grad_y, u_gate, u_up, w_gate, w_up, w_down, x_in, gamma, grad_res, attn_out, w_out):
        own, hidden = x_norm.shape
        tokens, ffn = u_gate.shape
        cols = attn_out.shape[1]
        anywhere = pl.BlockSpec(memory_space=pl.ANY)
        shape = jax.ShapeDtypeStruct
        dma = pltpu.SemaphoreType.DMA
        outs = pl.pallas_call(
            kernel,
            out_shape=[
                shape((own, hidden), BF16), shape((tokens, cols), BF16),
                shape((hidden, ffn), F32), shape((hidden, ffn), F32), shape((ffn, hidden), F32),
                shape((cols, hidden), F32),
                shape((tokens, hidden), BF16), shape((tokens, hidden), BF16), shape((tokens, hidden), BF16),
            ],
            in_specs=[anywhere] * 8 + [pl.BlockSpec(memory_space=pltpu.VMEM)] + [anywhere] * 3,
            out_specs=[anywhere] * 9,
            scratch_shapes=[
                pltpu.VMEM((hidden, ffn), BF16), pltpu.VMEM((hidden, ffn), BF16), pltpu.VMEM((ffn, hidden), BF16),
                pltpu.VMEM((hidden, ffn), F32), pltpu.VMEM((hidden, ffn), F32), pltpu.VMEM((ffn, hidden), F32),
                pltpu.VMEM((ROWS, hidden), BF16), pltpu.VMEM((ROWS, hidden), BF16),
                pltpu.VMEM((ROWS, ffn), BF16), pltpu.VMEM((ROWS, ffn), BF16),
                pltpu.VMEM((ROWS, ffn), BF16), pltpu.VMEM((ROWS, ffn), BF16), pltpu.VMEM((ROWS, ffn), BF16),
                pltpu.VMEM((ffn, ROWS), BF16), pltpu.VMEM((hidden, ROWS), BF16),
                pltpu.VMEM((own, hidden), F32), pltpu.VMEM((own, hidden), BF16), pltpu.VMEM((2, own, hidden), BF16),
                pltpu.VMEM((2, 2, QUARTER, hidden), BF16), pltpu.VMEM((3, 2, QUARTER, hidden), BF16),
                pltpu.VMEM((own, hidden), F32),
                pltpu.VMEM((tokens, cols), BF16), pltpu.VMEM((cols, hidden), BF16),
                pltpu.VMEM((tokens, cols), BF16), pltpu.VMEM((cols, hidden), F32),
                dma((CHIPS, 2)), dma((CHIPS, 2)), dma((CHIPS, 2)), dma((CHIPS, 2)),
                dma((CHIPS, 2)), dma((CHIPS, 2)), dma((CHIPS, 2)), dma((CHIPS, 2)),
                dma((CHIPS, 4)), dma((CHIPS, 4)), dma((CHIPS, 4)), dma((CHIPS, 4)),
                dma, dma((2,)), dma((2, 2)), dma((3, 2)),
                dma((5,)), dma((4,)), dma((4,)), dma((4,)), dma((4,)), dma((6,)),
            ],
            compiler_params=pltpu.CompilerParams(
                collective_id=0, has_side_effects=True, vmem_limit_bytes=67_043_328),
            name="mlp_backward",
        )(x_norm, grad_y, u_gate, u_up, w_gate, w_up, w_down, x_in, gamma.reshape(1, hidden), grad_res,
          attn_out, w_out)
        return tuple(outs[:6])

    return jax.shard_map(
        local_backward,
        mesh=mesh,
        in_specs=(token_spec, token_spec, split_cols, split_cols, weight_cols, weight_cols, weight_rows,
                  token_spec, P(None), token_spec, split_cols, weight_rows),
        out_specs=(token_spec, split_cols, split_cols, split_cols, token_spec, token_spec),
        check_vma=False,
    )
```

time: 665 us -> 382 us (0.57)
  waiting for transfers between devices: 494 us -> 0 us
  Pallas kernels: 0 us -> 333 us
  matrix products: 150 us -> 0 us
  local copies, waits for them, and re-layouts: 2.73 us -> 47 us
  between operations: 13.8 us -> 0.66 us
    pallas_call x0 -> x1, Pallas kernels: none -> 333 us  [local_backward(): pl.pallas_call(kernel, out_shape=[shape((own, hidden), BF16), shape((toke...]
    all_gather x3 -> x0, waiting for transfers between devices: 319 us -> none  [the longest x1 131 us: local_backward(): gy_full = lax.all_gather(grad_y, 'tp', axis=0, tiled=True)]
    reduce_scatter x1 -> x0, waiting for transfers between devices: 174 us -> none  [local_backward(): lax.psum_scatter(part_x.astype(jnp.bfloat16), 'tp', scatter_dimension=0,...]
    dot_general x8 -> x0, matrix products: 150 us -> none  [the longest x1 25.1 us: local_backward(): lax.dot_general(grad_up, w_up, CONTRACT_COLS, preferred_element_type=jnp....]
    unnamed x21 -> x18, local copies, waits for them, and re-layouts: 2.73 us -> 45.6 us
  transfers between devices with their start and end apart: 4 -> 0, of which waited for: 4 -> 0; matrix products, arithmetic and copies ran while one was open for 10% -> 0% of each run, Pallas kernels for 0% -> 0%
where the time goes in v1:
time: 382 us; the launch traced here: 381 us
  Pallas kernels  333 us (87%)
  local copies, waits for them, and re-layouts  47 us (12%)
    pallas_call x1, Pallas kernels, local_backward(): pl.pallas_call(kernel, out_shape=[shape((own, hidden), BF16), shape((toke...  333 us
    unnamed x18, local copies, waits for them, and re-layouts  45.6 us

profile of v1, /device:TPU:0, one launch (start us, length us, event | category | flops | bytes accessed | tf_op | source)
XLA Modules:
  0.0 380.7 jit_solution(15008353470380920184)
XLA Ops:
  0.6 0.0 copy-start
  0.6 1.4 reshape.15.gamma
  2.1 4.6 %copy.20.wg = bf16[2048,688]{1,0:T(8,128)(2,1)} copy(bf16[2048,688]{0,1:T(8,128)(2,1)} %param.16) | data formatting | bytes 5636096 | tf_op args[4]
  6.7 0.0 copy-done
  6.7 2.8 copy.21.wu
  9.4 8.4 %copy.18.ug = bf16[4096,688]{1,0:T(8,128)(2,1)} copy(bf16[4096,688]{0,1:T(8,128)(2,1)} %param.14) | data formatting | bytes 11272192 | tf_op args[2]
  17.8 8.3 %copy.19.uu = bf16[4096,688]{1,0:T(8,128)(2,1)} copy(bf16[4096,688]{0,1:T(8,128)(2,1)} %param.15) | data formatting | bytes 11272192 | tf_op args[3]
  26.1 333.0 %mlp_backward.1 = (bf16[256,2048]{1,0:T(8,128)(2,1)}, bf16[4096,128]{1,0:T(8,128)(2,1)}, f32[2048,688]{1,0:T(8,128)}, f32[2048,688]{1,0:T(8,128)}, f32[688,2048]...) custom-call(bf16[256,2048]{1,0:T(8,128)(2,1)} %x.1, ...), custom_call_target="tpu_custom_call" | custom-call | tf_op jit(solution)/shard_map/mlp_backward/pallas_call | solution.py:411
  359.1 6.3 %copy.22 = f32[2048,688]{0,1:T(8,128)} copy(f32[2048,688]{1,0:T(8,128)} %get-tuple-element.20) | data formatting | bytes 11272192
  365.4 0.0 copy-start.3
  365.4 0.0 copy-start.2
  365.4 6.5 %copy.23 = f32[2048,688]{0,1:T(8,128)} copy(f32[2048,688]{1,0:T(8,128)} %get-tuple-element.21) | data formatting | bytes 11272192
  371.9 0.0 copy-done.3
  371.9 1.0 copy.28
  372.9 0.0 copy-done.2
  372.9 1.0 copy.29
  373.8 0.0 copy-start.1
  373.8 5.9 %copy.30 = f32[688,2048]{1,0:T(8,128)} copy(f32[688,2048]{1,0:T(8,128)} %get-tuple-element.34) | data formatting | bytes 11272192
  379.7 0.0 copy-done.1
  379.7 1.0 copy.31
Async XLA Ops:
  0.6 6.0 %copy-start = (bf16[2048,688]{0,1:T(8,128)(2,1)S(1)}, bf16[2048,688]{0,1:T(8,128)(2,1)}, u32[]{:S(2)}) copy-start(bf16[2048,688]{0,1:T(8,128)(2,1)} %param.17) | copy-start | bytes 8454148
  365.4 6.5 %copy-start.3 = (bf16[256,2048]{1,0:T(8,128)(2,1)S(1)}, bf16[256,2048]{1,0:T(8,128)(2,1)}, u32[]{:S(2)}) copy-start(bf16[256,2048]{1,0:T(8,128)(2,1)} %get-tuple-element.30) | copy-start | bytes 3145732
  365.4 7.4 %copy-start.2 = (bf16[4096,128]{1,0:T(8,128)(2,1)S(1)}, bf16[4096,128]{1,0:T(8,128)(2,1)}, u32[]{:S(2)}) copy-start(bf16[4096,128]{1,0:T(8,128)(2,1)} %get-tuple-element.31) | copy-start | bytes 3145732
  373.8 5.9 %copy-start.1 = (f32[128,2048]{1,0:T(8,128)S(1)}, f32[128,2048]{1,0:T(8,128)}, u32[]{:S(2)}) copy-start(f32[128,2048]{1,0:T(8,128)} %get-tuple-element.35) | copy-start | bytes 3145732

commit v2 on v1

--- a/solution.py
+++ b/solution.py
@@ -26,14 +26,14 @@
 
 
 def kernel(x, gy, ug, uu, wg, wu, wd, xin, gamma, gres, att, wo,
-           out_ds, out_do, out_wg, out_wu, out_wd, out_wo, gy_all, x_all, ds_all,
-           wg_v, wu_v, wd_v, acc_g, acc_u, acc_d,
-           gy_b, x_b, ug_b, uu_b, z_b, dg_b, du_b, zt_b, xt_b,
+           out_ds, do_v, acc_g, acc_u, acc_d, acc_o, gy_all, x_all, ds_all,
+           wg_v, wu_v, wd_v,
+           gy_b, x_b, ug_b, uu_b, z_b, dg_b, du_b, dgt_b, dut_b,
            p_own, p_send, p_recv, rs_send, rs_recv, own_sum,
-           att_v, wo_v, do_v, acc_o,
+           att_v, wo_v,
            gy_ss, gy_rs, gy_ps, gy_pr, x_ss, x_rs, x_ps, x_pr,
            ds_ss, ds_rs, ds_ps, ds_pr, ps_sem, pr_sem, rss_sem, rsr_sem,
-           w_sem, gy_sem, x_sem, ug_sem, uu_sem, o_sem):
+           w_sem, gy_sem, x_sem, ug_sem, uu_sem):
     hidden = gy.shape[1]
     t = lax.axis_index("tp")
     core = t % 2
@@ -103,8 +103,8 @@
                 c = core if k == 0 else 1 - core
                 rows = pl.ds(row(s, d, c), QUARTER)
                 at = pl.ds((2 * k + d) * QUARTER, QUARTER)
-                copies.append(pltpu.make_async_copy(ug.at[rows, :], ug_b.at[at, :], ug_sem.at[2 * k + d]))
-                copies.append(pltpu.make_async_copy(uu.at[rows, :], uu_b.at[at, :], uu_sem.at[2 * k + d]))
+                copies.append(pltpu.make_async_copy(ug.at[:, rows], ug_b.at[:, at], ug_sem.at[2 * k + d]))
+                copies.append(pltpu.make_async_copy(uu.at[:, rows], uu_b.at[:, at], uu_sem.at[2 * k + d]))
         return copies
 
     for copy in load_u(0):
@@ -174,17 +174,21 @@
         landed(gy_all, gy_b, gy_sem, s)
 
         def hidden_tile(i, carry):
-            at = pl.ds(pl.multiple_of(i * 128, 128), 128)
-            grad_h = dot_cols(gy_b[at, :], wd_v[...])
-            gate = ug_b[at, :].astype(F32)
-            up = uu_b[at, :].astype(F32)
+            at = pl.ds(pl.multiple_of(i * 256, 256), 256)
+            grad_h = dot_cols(wd_v[...], gy_b[at, :])
+            gate = ug_b[:, at].astype(F32)
+            up = uu_b[:, at].astype(F32)
             sig = jax.nn.sigmoid(gate)
             act = gate * sig
-            z_b[at, :] = (act * up).astype(BF16)
-            du_b[at, :] = (grad_h * act).astype(BF16)
-            dg_b[at, :] = (grad_h * up * (sig * (1.0 + gate * (1.0 - sig)))).astype(BF16)
+            z_b[:, at] = (act * up).astype(BF16)
+            grad_up = (grad_h * act).astype(BF16)
+            grad_gate = (grad_h * up * (sig * (1.0 + gate * (1.0 - sig)))).astype(BF16)
+            du_b[:, at] = grad_up
+            dg_b[:, at] = grad_gate
+            dut_b[at, :] = grad_up.T
+            dgt_b[at, :] = grad_gate.T
             return carry
-        lax.fori_loop(0, ROWS // 128, hidden_tile, 0)
+        lax.fori_loop(0, ROWS // 256, hidden_tile, 0)
 
         @pl.when(s < LAST)
         def _():
@@ -197,7 +201,7 @@
 
         def part_tile(j, carry):
             at = pl.ds(pl.multiple_of(j * 512, 512), 512)
-            part = dot_cols(dg_b[...], wg_v[at, :]) + dot_cols(du_b[...], wu_v[at, :])
+            part = dot_plain(dgt_b[...], wg_v[:, at]) + dot_plain(dut_b[...], wu_v[:, at])
             p_own[:, at] = part[:2 * QUARTER]
             p_send[:, at] = part[2 * QUARTER:].astype(BF16)
             return carry
@@ -205,12 +209,6 @@
         swap(s).start()
 
         receive(streams[1], x_b, x_sem, s)
-
-        def zt_tile(i, carry):
-            at = pl.ds(pl.multiple_of(i * 128, 128), 128)
-            zt_b[:, at] = z_b[at, :].T
-            return carry
-        lax.fori_loop(0, ROWS // 128, zt_tile, 0)
 
         swap(s).wait_recv()
 
@@ -245,32 +243,21 @@
 
         def down_tile(j, carry):
             at = pl.ds(pl.multiple_of(j * 512, 512), 512)
-            acc_d[:, at] += dot_plain(zt_b[...], gy_b[:, at])
+            acc_d[:, at] += dot_plain(z_b[...], gy_b[:, at])
             return carry
         lax.fori_loop(0, hidden // 512, down_tile, 0)
 
         landed(x_all, x_b, x_sem, s)
 
-        def xt_tile(i, carry):
-            at = pl.ds(pl.multiple_of(i * 128, 128), 128)
-            xt_b[at, :] = x_b[:, at].T
-            return carry
-        lax.fori_loop(0, hidden // 128, xt_tile, 0)
-
-        def up_tile(i, carry):
-            at = pl.ds(pl.multiple_of(i * 512, 512), 512)
-            acc_g[at, :] += dot_plain(xt_b[at, :], dg_b[...])
-            acc_u[at, :] += dot_plain(xt_b[at, :], du_b[...])
+        def up_tile(j, carry):
+            at = pl.ds(pl.multiple_of(j * 512, 512), 512)
+            acc_g[:, at] += dot_plain(dg_b[...], x_b[:, at])
+            acc_u[:, at] += dot_plain(du_b[...], x_b[:, at])
             return carry
         lax.fori_loop(0, hidden // 512, up_tile, 0)
         return carry
 
     lax.fori_loop(0, CHIPS, step, 0)
-
-    stores = [pltpu.make_async_copy(a, b, o_sem.at[i]) for i, (a, b) in enumerate(
-        ((acc_g, out_wg), (acc_u, out_wu), (acc_d, out_wd)))]
-    for copy in stores:
-        copy.start()
 
     norm_loads = [pltpu.make_async_copy(src, x_b.at[pl.ds(k * 2 * QUARTER, 2 * QUARTER), :], x_sem.at[k])
                   for k, src in enumerate((xin, gres))]
@@ -300,7 +287,7 @@
         return remote(ds_all.at[rows, :], ds_all.at[rows, :],
                       ds_ps.at[s, 2 * d + h], ds_pr.at[s, 2 * d + h], twin)
 
-    gain = gamma[...].astype(F32)
+    gain = gamma[...].astype(F32)[None, :]
     for d in (0, 1):
         sum_in(CHIPS, d).wait_recv()
     for h in (0, 1):
@@ -316,15 +303,13 @@
                 proj = jnp.mean(scaled * xin_f, axis=-1, keepdims=True)
                 grad_s = (x_b[skip, :].astype(F32)
                           + inv_rms * (scaled - xin_f * (inv_rms * inv_rms) * proj)).astype(BF16)
-                p_send[here, :] = grad_s
+                out_ds[here, :] = grad_s
                 gy_b[here, :] = grad_s
                 return carry
             lax.fori_loop(0, HALF // 16, norm_tile, 0)
-            mine = p_send.at[pl.ds(d * QUARTER + h * HALF, HALF), :]
+            mine = out_ds.at[pl.ds(d * QUARTER + h * HALF, HALF), :]
             ds_next(1, d, h, mine).start()
             ds_twin(0, d, h, mine).start()
-    store_ds = pltpu.make_async_copy(p_send, out_ds, o_sem.at[3])
-    store_ds.start()
 
     def project(s):
         for d in (0, 1):
@@ -338,14 +323,14 @@
                 c = core if k == 0 else 1 - core
                 rows = pl.ds(row(s, d, c), QUARTER)
                 at = pl.ds((2 * k + d) * QUARTER, QUARTER)
-                zt_b[pl.ds(0, QUARTER), at] = att_v[rows, :].T
+                z_b[pl.ds(0, QUARTER), at] = att_v[rows, :].T
         grad_o = dot_cols(gy_b[...], wo_v[...]).astype(BF16)
         for k in (0, 1):
             for d in (0, 1):
                 c = core if k == 0 else 1 - core
                 do_v[pl.ds(row(s, d, c), QUARTER), :] = grad_o[(2 * k + d) * QUARTER:(2 * k + d + 1) * QUARTER]
         for j in range(0, hidden, 512):
-            acc_o[:, j:j + 512] += dot_plain(zt_b[pl.ds(0, QUARTER), :], gy_b[:, j:j + 512])
+            acc_o[:, j:j + 512] += dot_plain(z_b[pl.ds(0, QUARTER), :], gy_b[:, j:j + 512])
 
     def ds_relay(s, h):
         for d in (0, 1):
@@ -368,10 +353,6 @@
 
     lax.fori_loop(1, CHIPS, ds_step, 0)
     project(LAST)
-
-    last = [pltpu.make_async_copy(do_v, out_do, o_sem.at[4]), pltpu.make_async_copy(acc_o, out_wo, o_sem.at[5])]
-    for copy in last:
-        copy.start()
 
     def drain(s, carry):
         for d in (0, 1):
@@ -391,8 +372,6 @@
     for d in (0, 1):
         sum_on(LAST - 1, d).wait_send()
         sum_on(LAST, d).wait_send()
-    for copy in stores + [store_ds] + last:
-        copy.wait()
 
 
 def solution(mesh):
@@ -406,42 +385,41 @@
         tokens, ffn = u_gate.shape
         cols = attn_out.shape[1]
         anywhere = pl.BlockSpec(memory_space=pl.ANY)
+        inside = pl.BlockSpec(memory_space=pltpu.VMEM)
         shape = jax.ShapeDtypeStruct
         dma = pltpu.SemaphoreType.DMA
         outs = pl.pallas_call(
             kernel,
             out_shape=[
-                shape((own, hidden), BF16), shape((tokens, cols), BF16),
-                shape((hidden, ffn), F32), shape((hidden, ffn), F32), shape((ffn, hidden), F32),
-                shape((cols, hidden), F32),
+                pltpu.VMEM((own, hidden), BF16), pltpu.VMEM((tokens, cols), BF16),
+                pltpu.VMEM((ffn, hidden), F32), pltpu.VMEM((ffn, hidden), F32), pltpu.VMEM((ffn, hidden), F32),
+                pltpu.VMEM((cols, hidden), F32),
                 shape((tokens, hidden), BF16), shape((tokens, hidden), BF16), shape((tokens, hidden), BF16),
             ],
-            in_specs=[anywhere] * 8 + [pl.BlockSpec(memory_space=pltpu.VMEM)] + [anywhere] * 3,
-            out_specs=[anywhere] * 9,
+            in_specs=[anywhere] * 8 + [inside] + [anywhere] * 3,
+            out_specs=[inside] * 6 + [anywhere] * 3,
             scratch_shapes=[
-                pltpu.VMEM((hidden, ffn), BF16), pltpu.VMEM((hidden, ffn), BF16), pltpu.VMEM((ffn, hidden), BF16),
-                pltpu.VMEM((hidden, ffn), F32), pltpu.VMEM((hidden, ffn), F32), pltpu.VMEM((ffn, hidden), F32),
+                pltpu.VMEM((ffn, hidden), BF16), pltpu.VMEM((ffn, hidden), BF16), pltpu.VMEM((ffn, hidden), BF16),
                 pltpu.VMEM((ROWS, hidden), BF16), pltpu.VMEM((ROWS, hidden), BF16),
+                pltpu.VMEM((ffn, ROWS), BF16), pltpu.VMEM((ffn, ROWS), BF16),
+                pltpu.VMEM((ffn, ROWS), BF16), pltpu.VMEM((ffn, ROWS), BF16), pltpu.VMEM((ffn, ROWS), BF16),
                 pltpu.VMEM((ROWS, ffn), BF16), pltpu.VMEM((ROWS, ffn), BF16),
-                pltpu.VMEM((ROWS, ffn), BF16), pltpu.VMEM((ROWS, ffn), BF16), pltpu.VMEM((ROWS, ffn), BF16),
-                pltpu.VMEM((ffn, ROWS), BF16), pltpu.VMEM((hidden, ROWS), BF16),
                 pltpu.VMEM((own, hidden), F32), pltpu.VMEM((own, hidden), BF16), pltpu.VMEM((2, own, hidden), BF16),
                 pltpu.VMEM((2, 2, QUARTER, hidden), BF16), pltpu.VMEM((3, 2, QUARTER, hidden), BF16),
                 pltpu.VMEM((own, hidden), F32),
                 pltpu.VMEM((tokens, cols), BF16), pltpu.VMEM((cols, hidden), BF16),
-                pltpu.VMEM((tokens, cols), BF16), pltpu.VMEM((cols, hidden), F32),
                 dma((CHIPS, 2)), dma((CHIPS, 2)), dma((CHIPS, 2)), dma((CHIPS, 2)),
                 dma((CHIPS, 2)), dma((CHIPS, 2)), dma((CHIPS, 2)), dma((CHIPS, 2)),
                 dma((CHIPS, 4)), dma((CHIPS, 4)), dma((CHIPS, 4)), dma((CHIPS, 4)),
                 dma, dma((2,)), dma((2, 2)), dma((3, 2)),
-                dma((5,)), dma((4,)), dma((4,)), dma((4,)), dma((4,)), dma((6,)),
+                dma((5,)), dma((4,)), dma((4,)), dma((4,)), dma((4,)),
             ],
             compiler_params=pltpu.CompilerParams(
-                collective_id=0, has_side_effects=True, vmem_limit_bytes=67_043_328),
+                collective_id=0, has_side_effects=True, vmem_limit_bytes=44 * 2 ** 20),
             name="mlp_backward",
-        )(x_norm, grad_y, u_gate, u_up, w_gate, w_up, w_down, x_in, gamma.reshape(1, hidden), grad_res,
-          attn_out, w_out)
-        return tuple(outs[:6])
+        )(x_norm, grad_y, u_gate.T, u_up.T, w_gate.T, w_up.T, w_down, x_in, gamma, grad_res, attn_out, w_out)
+        grad_sum, grad_attn, gw_gate, gw_up, gw_down, gw_out = outs[:6]
+        return grad_sum, grad_attn, gw_gate.T, gw_up.T, gw_down, gw_out
 
     return jax.shard_map(
         local_backward,

time: 382 us -> 342 us (0.90)
  local copies, waits for them, and re-layouts: 47 us -> 10.4 us
    unnamed x18 -> x6, local copies, waits for them, and re-layouts: 45.6 us -> 10.4 us
where the time goes in v2:
time: 342 us; the launch traced here: 341 us
  Pallas kernels  330 us (96%)
  local copies, waits for them, and re-layouts  10.4 us (3%)
    pallas_call x1, Pallas kernels, local_backward(): pl.pallas_call(kernel, out_shape=[pltpu.VMEM((own, hidden), BF16), pltpu....  330 us
    unnamed x6, local copies, waits for them, and re-layouts  10.4 us

profile of v2, /device:TPU:0, one launch (start us, length us, event | category | flops | bytes accessed | tf_op | source)
XLA Modules:
  0.0 341.1 jit_solution(16197439547740817600)
XLA Ops:
  0.6 330.1 %mlp_backward.1 = (bf16[256,2048]{1,0:T(8,128)(2,1)S(1)}, bf16[4096,128]{1,0:T(8,128)(2,1)S(1)}, f32[688,2048]{1,0:T(8,128)S(1)}, f32[688,2048]{1,0:T(8,128)S(1)...) custom-call(bf16[256,2048]{1,0:T(8,128)(2,1)} %x.1, ...), custom_call_target="tpu_custom_call" | custom-call | tf_op jit(solution)/shard_map/mlp_backward/pallas_call | solution.py:391
  330.7 1.0 copy.24
  331.7 1.0 copy.25
  332.7 1.0 copy.29
  333.6 2.5 copy.26
  336.1 2.5 copy.27
  338.6 2.5 copy.28

commit v3 on v2

v3 whole, which is shorter than its diff:
```python
import jax
import jax.numpy as jnp
from jax import lax
from jax.experimental import pallas as pl
from jax.experimental.pallas import tpu as pltpu
from jax.sharding import PartitionSpec as P

NORM_EPS = 1e-5
MESH = pl.DeviceIdType.MESH
BF16 = jnp.bfloat16
F32 = jnp.float32

CHIPS = 8
QUARTER = 128
HALF = 64
ROWS = 4 * QUARTER
LAST = CHIPS - 1


def dot_cols(a, b):
    return lax.dot_general(a, b, (((1,), (1,)), ((), ())), preferred_element_type=F32)


def dot_plain(a, b):
    return lax.dot_general(a, b, (((1,), (0,)), ((), ())), preferred_element_type=F32)


def kernel(x, gy, ug, uu, wg, wu, wd, xin, gamma, gres, att, wo,
           out_ds, do_v, acc_g, acc_u, acc_d, acc_o, gy_all, x_all, ds_all, rs_in, z_all, dg_all, du_all,
           wg_v, wu_v, wd_v,
           gy_b, x_b, ug_b, uu_b, z_b, dg_b, du_b, dgt_b, dut_b,
           p_own, p_send, p_recv, hold, own_sum, stage, y_in,
           att_v, wo_v,
           gy_zs, gy_zr, gy_ys, gy_yr, gy_ts, gy_tr, x_zs, x_zr, x_ys, x_yr, x_ts, x_tr,
           ds_ss, ds_rs, ds_ps, ds_pr, ps_sem, pr_sem, rss_sem, rsr_sem, yss_sem, ysr_sem,
           w_sem, gy_sem, x_sem, u_sem, keep_sem, stage_sem):
    hidden = gy.shape[1]
    own = gy.shape[0]
    t = lax.axis_index("tp")
    core = t % 2
    y = (t // 2) % 2
    z = t // 4
    edge = z % 3 == 0
    inner = z % 3 != 0
    pos = z + y * (7 - 2 * z)

    def device(chip, c):
        upper = chip // 4
        return 4 * (chip + upper * (7 - 2 * chip)) + 2 * upper + c

    onward = (device((pos + 1) % CHIPS, core), device((pos + LAST) % CHIPS, core))
    twin = t + 1 - 2 * core
    over = t + 2 - 4 * y
    beside = (t + 4 - 4 * (z // 3), t - 4 + 4 * ((3 - z) // 3))

    def signal(other):
        pl.semaphore_signal(barrier, inc=1, device_id={"tp": other}, device_id_type=MESH)

    barrier = pltpu.get_barrier_semaphore()
    signal(over)
    signal(twin)

    @pl.when(z < 3)
    def _():
        signal(beside[0])

    @pl.when(z > 0)
    def _():
        signal(beside[1])

    @pl.when(edge)
    def _():
        pl.semaphore_wait(barrier, 3)

    @pl.when(inner)
    def _():
        pl.semaphore_wait(barrier, 4)

    def remote(src, dst, send, recv, to):
        return pltpu.make_async_remote_copy(src_ref=src, dst_ref=dst, send_sem=send, recv_sem=recv,
                                            device_id={"tp": to}, device_id_type=MESH)

    def column(k):
        far = z // 2
        near = z + far * (3 - 2 * z)
        late = k // 2
        col = (1 - near) * k + near * ((1 - late) * (1 - k) + late * k)
        return col + far * (3 - 2 * col)

    def line(r):
        return y + r - 2 * y * r

    def first_row(col, r, c):
        return pl.multiple_of(((col * 2 + line(r)) * 2 + c) * own, own)

    def half(col, r, c, h):
        return pl.ds(pl.multiple_of(first_row(col, r, c) + h * QUARTER, QUARTER), QUARTER)

    class Stream:
        def __init__(self, own_ref, full, zs, zr, ys, yr, ts, tr):
            self.own, self.full = own_ref, full
            self.zs, self.zr, self.ys, self.yr, self.ts, self.tr = zs, zr, ys, yr, ts, tr

        def part(self, col, r, c, h):
            return self.full.at[half(col, r, c, h), :]

        def mine(self, h):
            return self.own.at[pl.ds(h * QUARTER, QUARTER), :]

        def along(self, col, h, side, src=None):
            dst = self.part(col, 0, core, h)
            return remote(dst if src is None else src, dst, self.zs.at[side, col, h], self.zr.at[col, h], beside[side])

        def across(self, col, h, src=None):
            dst = self.part(col, 0, core, h)
            return remote(dst if src is None else src, dst, self.ys.at[col, h], self.yr.at[col, h], over)

        def from_over(self, col, h):
            dst = self.part(col, 1, core, h)
            return remote(dst, dst, self.ys.at[col, h], self.yr.at[col, h], over)

        def hand(self, col, r, h, src=None):
            dst = self.part(col, r, core, h)
            return remote(dst if src is None else src, dst, self.ts.at[r, col, h], self.tr.at[r, col, h], twin)

        def from_twin(self, col, r, h):
            dst = self.part(col, r, 1 - core, h)
            return remote(dst, dst, self.ts.at[r, col, h], self.tr.at[r, col, h], twin)

        def relay_row(self, dist, h):
            @pl.when(z >= dist)
            def _():
                self.along(z - dist, h, 0).wait_recv()

                @pl.when(z < 3)
                def _():
                    self.along(z - dist, h, 0).start()
                self.across(z - dist, h).start()
                self.hand(z - dist, 0, h).start()

            @pl.when(z + dist < 4)
            def _():
                self.along(z + dist, h, 1).wait_recv()

                @pl.when(z > 0)
                def _():
                    self.along(z + dist, h, 1).start()
                self.across(z + dist, h).start()
                self.hand(z + dist, 0, h).start()

        def relay_over(self, k, h):
            self.from_over(column(k), h).wait_recv()
            self.hand(column(k), 1, h).start()

        def start_row(self):
            for h in (0, 1):
                @pl.when(z < 3)
                def _():
                    self.along(z, h, 0, self.mine(h)).start()

                @pl.when(z > 0)
                def _():
                    self.along(z, h, 1, self.mine(h)).start()

        def start_rest(self):
            for h in (0, 1):
                self.across(z, h, self.mine(h)).start()
                self.hand(z, 0, h, self.mine(h)).start()

        def load(self, n, buf, sem):
            k, r = n // 2, n % 2

            @pl.when(n == 0)
            def _():
                pltpu.make_async_copy(self.own, buf.at[pl.ds(0, own), :], sem.at[0]).start()

            @pl.when(n > 0)
            def _():
                self.block(n, core, buf, sem, 0).start()
            for h in (0, 1):
                self.from_twin(column(k), r, h).wait_recv()
            self.block(n, 1 - core, buf, sem, 1).start()

        def block(self, n, c, buf, sem, i):
            rows = pl.ds(first_row(column(n // 2), n % 2, c), own)
            return pltpu.make_async_copy(self.full.at[rows, :], buf.at[pl.ds(i * own, own), :], sem.at[i])

        def landed(self, n, buf, sem):
            for i in (0, 1):
                self.block(n, core, buf, sem, i).wait()

        def drain(self, col):
            for h in (0, 1):
                self.across(col, h).wait_send()
                for r in (0, 1):
                    self.hand(col, r, h).wait_send()

                @pl.when((z < 3) & (col <= z))
                def _():
                    self.along(col, h, 0).wait_send()

                @pl.when((z > 0) & (col >= z))
                def _():
                    self.along(col, h, 1).wait_send()

    gys = Stream(gy, gy_all, gy_zs, gy_zr, gy_ys, gy_yr, gy_ts, gy_tr)
    xs = Stream(x, x_all, x_zs, x_zr, x_ys, x_yr, x_ts, x_tr)
    gys.start_row()
    gys.start_rest()

    @pl.when(edge)
    def _():
        xs.start_row()

    loads = [pltpu.make_async_copy(a, b, w_sem.at[i]) for i, (a, b) in enumerate(
        ((wd, wd_v), (wg, wg_v), (wu, wu_v), (att, att_v), (wo, wo_v)))]
    for copy in loads:
        copy.start()

    def load_u(n):
        copies = []
        for i in (0, 1):
            c = core if i == 0 else 1 - core
            rows = pl.ds(first_row(column(n // 2), n % 2, c), own)
            at = pl.ds(i * own, own)
            copies.append(pltpu.make_async_copy(ug.at[:, rows], ug_b.at[:, at], u_sem.at[i]))
            copies.append(pltpu.make_async_copy(uu.at[:, rows], uu_b.at[:, at], u_sem.at[2 + i]))
        return copies

    for copy in load_u(0):
        copy.start()

    acc_g[...] = jnp.zeros_like(acc_g)
    acc_u[...] = jnp.zeros_like(acc_u)
    acc_d[...] = jnp.zeros_like(acc_d)
    acc_o[...] = jnp.zeros_like(acc_o)

    def keep(n):
        return [pltpu.make_async_copy(a, b.at[n], keep_sem.at[i])
                for i, (a, b) in enumerate(((z_b, z_all), (dg_b, dg_all), (du_b, du_all)))]

    def swap(n):
        return remote(p_send, p_recv.at[n % 2], ps_sem, pr_sem.at[n % 2], twin)

    def rs_slot(side, col, r, h):
        rows = pl.multiple_of((((side * 4 + col) * 2 + line(r)) * 2 + h) * QUARTER, QUARTER)
        return rs_in.at[pl.ds(rows, QUARTER), :], rsr_sem.at[side, col, line(r), h]

    def send_sum(k, r, h):
        col = column(k)
        up = (col - z + 3) // 4
        dst, sem = rs_slot(1 - up, col, r, h)
        return remote(hold.at[(k - 1) * 2 + r, pl.ds(h * QUARTER, QUARTER), :], dst,
                      rss_sem.at[k - 1, r, h], sem, t - 4 + 8 * up)

    def take_sum(side, col, r, h, slot):
        src, sem = rs_slot(side, col, r, h)
        remote(stage.at[slot], src, rss_sem.at[0, 0, 0], sem, twin).wait_recv()
        copy = pltpu.make_async_copy(src, stage.at[slot], stage_sem.at[slot])
        copy.start()
        return copy

    def finish(n):
        k, r = n // 2, n % 2
        swap(n).wait_recv()

        @pl.when(k == 0)
        def _():
            def tile(i, carry):
                at = pl.ds(pl.multiple_of(i * 32, 32), 32)
                own_sum[r, at, :] = p_own[at, :] + p_recv[n % 2, at, :].astype(F32)
                return carry
            lax.fori_loop(0, own // 32, tile, 0)

        @pl.when(k > 0)
        def _():
            def tile(i, carry):
                at = pl.ds(pl.multiple_of(i * 32, 32), 32)
                hold[(k - 1) * 2 + r, at, :] = (p_own[at, :] + p_recv[n % 2, at, :].astype(F32)).astype(BF16)
                return carry
            lax.fori_loop(0, own // 32, tile, 0)

            @pl.when(edge & (k == 1))
            def _():
                for h in (0, 1):
                    send_sum(k, r, h).start()

            @pl.when(edge & (k > 1) & (r == 1))
            def _():
                for q in (1, 0):
                    for h in (0, 1):
                        send_sum(k, q, h).start()

    def hidden_step(n, carry):
        k, h = n // 2, n % 2
        gys.relay_row(k + 1, h)
        gys.relay_over(k, h)

        @pl.when(n > 0)
        def _():
            finish(n - 1)

        @pl.when(inner & (n == 4))
        def _():
            xs.start_row()

        @pl.when(n == 6)
        def _():
            xs.start_rest()
            for q in (0, 1):
                xs.relay_row(1, q)

        gys.load(n, gy_b, gy_sem)
        for copy in load_u(n):
            copy.wait()

        @pl.when(n == 0)
        def _():
            for copy in loads:
                copy.wait()

        @pl.when(n > 0)
        def _():
            for copy in keep(n - 1):
                copy.wait()
            swap(n - 1).wait_send()
        gys.landed(n, gy_b, gy_sem)

        def hidden_tile(i, carry):
            at = pl.ds(pl.multiple_of(i * 256, 256), 256)
            grad_h = dot_cols(wd_v[...], gy_b[at, :])
            gate = ug_b[:, at].astype(F32)
            up = uu_b[:, at].astype(F32)
            sig = jax.nn.sigmoid(gate)
            act = gate * sig
            z_b[:, at] = (act * up).astype(BF16)
            grad_up = (grad_h * act).astype(BF16)
            grad_gate = (grad_h * up * (sig * (1.0 + gate * (1.0 - sig)))).astype(BF16)
            du_b[:, at] = grad_up
            dg_b[:, at] = grad_gate
            dut_b[at, :] = grad_up.T
            dgt_b[at, :] = grad_gate.T
            return carry
        lax.fori_loop(0, ROWS // 256, hidden_tile, 0)
        for copy in keep(n):
            copy.start()

        @pl.when(n < LAST)
        def _():
            for copy in load_u(n + 1):
                copy.start()

        def part_tile(j, carry):
            at = pl.ds(pl.multiple_of(j * 512, 512), 512)
            part = dot_plain(dgt_b[...], wg_v[:, at]) + dot_plain(dut_b[...], wu_v[:, at])
            p_own[:, at] = part[:own]
            p_send[:, at] = part[own:].astype(BF16)
            return carry
        lax.fori_loop(0, hidden // 512, part_tile, 0)
        swap(n).start()
        return carry

    lax.fori_loop(0, CHIPS, hidden_step, 0)
    finish(LAST)
    for copy in keep(LAST):
        copy.wait()
    swap(LAST).wait_send()

    def carry_on(k, m):
        r, h = 1 - m // 2, m % 2
        col = column(k)
        up = (col - z + 3) // 4
        take_sum(1 - up, col, r, h, m % 2).wait()
        base = h * QUARTER

        def tile(i, carry):
            at = pl.ds(pl.multiple_of(base + i * 32, 32), 32)
            here = pl.ds(pl.multiple_of(i * 32, 32), 32)
            total = hold[(k - 1) * 2 + r, at, :].astype(F32) + stage[m % 2, here, :].astype(F32)
            hold[(k - 1) * 2 + r, at, :] = total.astype(BF16)
            return carry
        lax.fori_loop(0, QUARTER // 32, tile, 0)
        send_sum(k, r, h).start()

    def settle(side, r):
        copies = [take_sum(side, z, r, h, h) for h in (0, 1)]
        for h in (0, 1):
            copies[h].wait()

            def tile(i, carry):
                at = pl.ds(pl.multiple_of(h * QUARTER + i * 32, 32), 32)
                here = pl.ds(pl.multiple_of(i * 32, 32), 32)
                own_sum[r, at, :] = own_sum[r, at, :] + stage[h, here, :].astype(F32)
                return carry
            lax.fori_loop(0, QUARTER // 32, tile, 0)

    def give(h):
        rows = pl.ds(h * QUARTER, QUARTER)
        return remote(p_send.at[rows, :], y_in.at[rows, :], yss_sem.at[h], ysr_sem.at[h], over)

    def give_over():
        for h in (0, 1):
            def tile(i, carry):
                at = pl.ds(pl.multiple_of(h * QUARTER + i * 32, 32), 32)
                p_send[at, :] = own_sum[1, at, :].astype(BF16)
                return carry
            lax.fori_loop(0, QUARTER // 32, tile, 0)
            give(h).start()

    def weight_step(n, carry):
        xs.load(n, x_b, x_sem)
        for i, c in ((0, core), (1, 1 - core)):
            @pl.when((n > 0) | (i == 1))
            def _():
                gys.block(n, c, gy_b, gy_sem, i).start()

        @pl.when(n == 0)
        def _():
            pltpu.make_async_copy(gy, gy_b.at[pl.ds(0, own), :], gy_sem.at[0]).start()
        back = [pltpu.make_async_copy(b.at[n], a, keep_sem.at[i])
                for i, (a, b) in enumerate(((z_b, z_all), (dg_b, dg_all), (du_b, du_all)))]
        for copy in back:
            copy.start()
        for copy in back:
            copy.wait()
        gys.landed(n, gy_b, gy_sem)
        xs.landed(n, x_b, x_sem)

        def tile(j, carry):
            at = pl.ds(pl.multiple_of(j * 512, 512), 512)
            acc_d[:, at] += dot_plain(z_b[...], gy_b[:, at])
            acc_g[:, at] += dot_plain(dg_b[...], x_b[:, at])
            acc_u[:, at] += dot_plain(du_b[...], x_b[:, at])
            return carry
        lax.fori_loop(0, hidden // 512, tile, 0)
        return carry

    def late_step(i, carry):
        for h in (0, 1):
            xs.relay_row(i + 2, h)

        @pl.when(inner & (i == 0))
        def _():
            for r in (0, 1):
                settle(z - 1, r)
            carry_on(2, 0)
            carry_on(2, 1)

        @pl.when(inner & (i == 1))
        def _():
            carry_on(2, 2)
            carry_on(2, 3)

        @pl.when(inner & (i == 2))
        def _():
            carry_on(3, 0)
        for h in (0, 1):
            xs.relay_over(i, h)

        @pl.when(inner & (i == 2))
        def _():
            settle(2 - z, 1)
            give_over()
            carry_on(3, 1)
            carry_on(1, 0)
            settle(2 - z, 0)
        lax.fori_loop(2 * i, 2 * i + 2, weight_step, 0)
        return carry

    lax.fori_loop(0, 3, late_step, 0)

    @pl.when(inner)
    def _():
        carry_on(3, 2)
        carry_on(1, 1)
    xs.relay_over(3, 0)

    @pl.when(inner)
    def _():
        carry_on(3, 3)
        carry_on(1, 2)
    xs.relay_over(3, 1)

    norm_loads = [pltpu.make_async_copy(src, x_b.at[pl.ds(k * own, own), :], x_sem.at[k])
                  for k, src in enumerate((xin, gres))]
    for copy in norm_loads:
        copy.start()

    @pl.when(inner)
    def _():
        carry_on(1, 3)

    @pl.when(edge)
    def _():
        settle((3 - z) // 3, 1)
        give_over()
        settle((3 - z) // 3, 0)
    for copy in norm_loads:
        copy.wait()

    def row(s, d, c):
        source = (pos + (CHIPS - s if d == 0 else s)) % CHIPS
        return pl.multiple_of(device(source, c) * 2 * QUARTER + d * QUARTER, QUARTER)

    def block_load(s, d, k):
        c = core if k == 0 else 1 - core
        at = pl.ds((2 * k + d) * QUARTER, QUARTER)
        return pltpu.make_async_copy(ds_all.at[pl.ds(row(s, d, c), QUARTER), :], gy_b.at[at, :], gy_sem.at[2 * k + d])

    def ds_next(s, d, h, src=None):
        rows = pl.ds(pl.multiple_of(row(s - 1, d, core) + h * HALF, HALF), HALF)
        return remote(ds_all.at[rows, :] if src is None else src, ds_all.at[rows, :],
                      ds_ss.at[s, 2 * d + h], ds_rs.at[s, 2 * d + h], onward[d])

    def ds_here(s, d, h):
        rows = pl.ds(pl.multiple_of(row(s, d, core) + h * HALF, HALF), HALF)
        return remote(ds_all.at[rows, :], ds_all.at[rows, :],
                      ds_ss.at[s, 2 * d + h], ds_rs.at[s, 2 * d + h], onward[d])

    def ds_twin(s, d, h, src=None):
        rows = pl.ds(pl.multiple_of(row(s, d, core) + h * HALF, HALF), HALF)
        return remote(ds_all.at[rows, :] if src is None else src, ds_all.at[rows, :],
                      ds_ps.at[s, 2 * d + h], ds_pr.at[s, 2 * d + h], twin)

    def ds_from_twin(s, d, h):
        rows = pl.ds(pl.multiple_of(row(s, d, 1 - core) + h * HALF, HALF), HALF)
        return remote(ds_all.at[rows, :], ds_all.at[rows, :],
                      ds_ps.at[s, 2 * d + h], ds_pr.at[s, 2 * d + h], twin)

    gain = gamma[...].astype(F32)[None, :]
    for d in (0, 1):
        give(d).wait_recv()
    for h in (0, 1):
        for d in (0, 1):
            def norm_tile(i, carry):
                here = pl.ds(pl.multiple_of(d * QUARTER + h * HALF + i * 16, 16), 16)
                skip = pl.ds(pl.multiple_of(2 * QUARTER + d * QUARTER + h * HALF + i * 16, 16), 16)
                grad_x = (own_sum[0, here, :] + y_in[here, :].astype(F32)).astype(BF16).astype(F32)
                xin_f = x_b[here, :].astype(F32)
                inv_rms = lax.rsqrt(jnp.mean(xin_f * xin_f, axis=-1, keepdims=True) + NORM_EPS)
                scaled = grad_x * gain
                proj = jnp.mean(scaled * xin_f, axis=-1, keepdims=True)
                grad_s = (x_b[skip, :].astype(F32)
                          + inv_rms * (scaled - xin_f * (inv_rms * inv_rms) * proj)).astype(BF16)
                out_ds[here, :] = grad_s
                return carry
            lax.fori_loop(0, HALF // 16, norm_tile, 0)
            mine = out_ds.at[pl.ds(d * QUARTER + h * HALF, HALF), :]
            ds_next(1, d, h, mine).start()
            ds_twin(0, d, h, mine).start()

    lax.fori_loop(6, 8, weight_step, 0)
    for d in (0, 1):
        gy_b[pl.ds(d * QUARTER, QUARTER), :] = out_ds[pl.ds(d * QUARTER, QUARTER), :]

    def project(s):
        for d in (0, 1):
            for h in (0, 1):
                ds_from_twin(s, d, h).wait_recv()
            block_load(s, d, 1).start()
        for d in (0, 1):
            block_load(s, d, 1).wait()
        for k in (0, 1):
            for d in (0, 1):
                c = core if k == 0 else 1 - core
                rows = pl.ds(row(s, d, c), QUARTER)
                at = pl.ds((2 * k + d) * QUARTER, QUARTER)
                z_b[pl.ds(0, QUARTER), at] = att_v[rows, :].T
        grad_o = dot_cols(gy_b[...], wo_v[...]).astype(BF16)
        for k in (0, 1):
            for d in (0, 1):
                c = core if k == 0 else 1 - core
                do_v[pl.ds(row(s, d, c), QUARTER), :] = grad_o[(2 * k + d) * QUARTER:(2 * k + d + 1) * QUARTER]
        for j in range(0, hidden, 512):
            acc_o[:, j:j + 512] += dot_plain(z_b[pl.ds(0, QUARTER), :], gy_b[:, j:j + 512])

    def ds_relay(s, h):
        for d in (0, 1):
            ds_here(s, d, h).wait_recv()

            @pl.when(s < LAST)
            def _():
                ds_next(s + 1, d, h).start()
            ds_twin(s, d, h).start()

    def ds_step(s, carry):
        ds_relay(s, 0)
        project(s - 1)
        ds_relay(s, 1)
        for d in (0, 1):
            block_load(s, d, 0).start()
        for d in (0, 1):
            block_load(s, d, 0).wait()
        return carry

    lax.fori_loop(1, CHIPS, ds_step, 0)
    project(LAST)

    def drain(s, carry):
        for d in (0, 1):
            for h in (0, 1):
                ds_twin(s, d, h).wait_send()

            @pl.when(s > 0)
            def _():
                for h in (0, 1):
                    ds_here(s, d, h).wait_send()
        return carry
    lax.fori_loop(0, CHIPS, drain, 0)

    def drain_columns(col, carry):
        gys.drain(col)
        xs.drain(col)

        @pl.when(col > 0)
        def _():
            for r in (0, 1):
                for h in (0, 1):
                    send_sum(col, r, h).wait_send()
        return carry
    lax.fori_loop(0, 4, drain_columns, 0)
    for h in (0, 1):
        give(h).wait_send()


def solution(mesh):
    token_spec = P(("dp", "tp"), None)
    split_cols = P("dp", "tp")
    weight_cols = P(None, "tp")
    weight_rows = P("tp", None)

    def local_backward(x_norm, grad_y, u_gate, u_up, w_gate, w_up, w_down, x_in, gamma, grad_res, attn_out, w_out):
        own, hidden = x_norm.shape
        tokens, ffn = u_gate.shape
        cols = attn_out.shape[1]
        anywhere = pl.BlockSpec(memory_space=pl.ANY)
        inside = pl.BlockSpec(memory_space=pltpu.VMEM)
        shape = jax.ShapeDtypeStruct
        dma = pltpu.SemaphoreType.DMA
        outs = pl.pallas_call(
            kernel,
            out_shape=[
                pltpu.VMEM((own, hidden), BF16), pltpu.VMEM((tokens, cols), BF16),
                pltpu.VMEM((ffn, hidden), F32), pltpu.VMEM((ffn, hidden), F32), pltpu.VMEM((ffn, hidden), F32),
                pltpu.VMEM((cols, hidden), F32),
                shape((tokens, hidden), BF16), shape((tokens, hidden), BF16), shape((tokens, hidden), BF16),
                shape((32 * QUARTER, hidden), BF16),
                shape((CHIPS, ffn, ROWS), BF16), shape((CHIPS, ffn, ROWS), BF16), shape((CHIPS, ffn, ROWS), BF16),
            ],
            in_specs=[anywhere] * 8 + [inside] + [anywhere] * 3,
            out_specs=[inside] * 6 + [anywhere] * 7,
            scratch_shapes=[
                pltpu.VMEM((ffn, hidden), BF16), pltpu.VMEM((ffn, hidden), BF16), pltpu.VMEM((ffn, hidden), BF16),
                pltpu.VMEM((ROWS, hidden), BF16), pltpu.VMEM((ROWS, hidden), BF16),
                pltpu.VMEM((ffn, ROWS), BF16), pltpu.VMEM((ffn, ROWS), BF16),
                pltpu.VMEM((ffn, ROWS), BF16), pltpu.VMEM((ffn, ROWS), BF16), pltpu.VMEM((ffn, ROWS), BF16),
                pltpu.VMEM((ROWS, ffn), BF16), pltpu.VMEM((ROWS, ffn), BF16),
                pltpu.VMEM((own, hidden), F32), pltpu.VMEM((own, hidden), BF16), pltpu.VMEM((2, own, hidden), BF16),
                pltpu.VMEM((6, own, hidden), BF16), pltpu.VMEM((2, own, hidden), F32),
                pltpu.VMEM((2, QUARTER, hidden), BF16), pltpu.VMEM((own, hidden), BF16),
                pltpu.VMEM((tokens, cols), BF16), pltpu.VMEM((cols, hidden), BF16),
                dma((2, 4, 2)), dma((4, 2)), dma((4, 2)), dma((4, 2)), dma((2, 4, 2)), dma((2, 4, 2)),
                dma((2, 4, 2)), dma((4, 2)), dma((4, 2)), dma((4, 2)), dma((2, 4, 2)), dma((2, 4, 2)),
                dma((CHIPS, 4)), dma((CHIPS, 4)), dma((CHIPS, 4)), dma((CHIPS, 4)),
                dma, dma((2,)), dma((3, 2, 2)), dma((2, 4, 2, 2)), dma((2,)), dma((2,)),
                dma((5,)), dma((4,)), dma((2,)), dma((4,)), dma((3,)), dma((2,)),
            ],
            compiler_params=pltpu.CompilerParams(
                collective_id=0, has_side_effects=True, vmem_limit_bytes=44 * 2 ** 20),
            name="mlp_backward",
        )(x_norm, grad_y, u_gate.T, u_up.T, w_gate.T, w_up.T, w_down, x_in, gamma, grad_res, attn_out, w_out)
        grad_sum, grad_attn, gw_gate, gw_up, gw_down, gw_out = outs[:6]
        return grad_sum, grad_attn, gw_gate.T, gw_up.T, gw_down, gw_out

    return jax.shard_map(
        local_backward,
        mesh=mesh,
        in_specs=(token_spec, token_spec, split_cols, split_cols, weight_cols, weight_cols, weight_rows,
                  token_spec, P(None), token_spec, split_cols, weight_rows),
        out_specs=(token_spec, split_cols, split_cols, split_cols, token_spec, token_spec),
        check_vma=False,
    )
```

time: 342 us -> 367 us (1.073)
  Pallas kernels: 330 us -> 354 us
    pallas_call x1, Pallas kernels: 330 us -> 354 us  [local_backward(): pl.pallas_call(kernel, out_shape=[pltpu.VMEM((own, hidden), BF16), pltpu....]
where the time goes in v3:
time: 367 us; the launch traced here: 365 us
  Pallas kernels  354 us (96%)
  local copies, waits for them, and re-layouts  10.4 us (3%)
    pallas_call x1, Pallas kernels, local_backward(): pl.pallas_call(kernel, out_shape=[pltpu.VMEM((own, hidden), BF16), pltpu....  354 us
    unnamed x6, local copies, waits for them, and re-layouts  10.4 us

profile of v3, /device:TPU:0, one launch (start us, length us, event | category | flops | bytes accessed | tf_op | source)
XLA Modules:
  0.0 365.1 jit_solution(13267165371080329982)
XLA Ops:
  0.6 354.1 %mlp_backward.1 = (bf16[256,2048]{1,0:T(8,128)(2,1)S(1)}, bf16[4096,128]{1,0:T(8,128)(2,1)S(1)}, f32[688,2048]{1,0:T(8,128)S(1)}, f32[688,2048]{1,0:T(8,128)S(1)...) custom-call(bf16[256,2048]{1,0:T(8,128)(2,1)} %x.1, ...), custom_call_target="tpu_custom_call" | custom-call | tf_op jit(solution)/shard_map/mlp_backward/pallas_call | solution.py:640
  354.7 1.0 copy.24
  355.7 1.0 copy.25
  356.6 1.0 copy.29
  357.6 2.5 copy.26
  360.1 2.5 copy.27
  362.6 2.5 copy.28

commit v4 on v3

--- a/solution.py
+++ b/solution.py
@@ -127,26 +127,37 @@
             dst = self.part(col, r, 1 - core, h)
             return remote(dst, dst, self.ts.at[r, col, h], self.tr.at[r, col, h], twin)
 
-        def relay_row(self, dist, h):
+        def relay(self, dist, h, side, held=False):
+            col = z - dist if side == 0 else z + dist
+            self.along(col, h, side).wait_recv()
+
+            @pl.when(z < 3 if side == 0 else z > 0)
+            def _():
+                self.along(col, h, side).start()
+            self.hand(col, 0, h).start()
+            if not held:
+                self.across(col, h).start()
+            else:
+                second = inner & (dist == 1) & (z == 2 - side)
+
+                @pl.when(jnp.logical_not(second))
+                def _():
+                    self.across(col, h).start()
+
+        def relay_row(self, dist, h, held=False):
             @pl.when(z >= dist)
             def _():
-                self.along(z - dist, h, 0).wait_recv()
-
-                @pl.when(z < 3)
+                self.relay(dist, h, 0, held)
+
+            @pl.when(z + dist < 4)
+            def _():
+                self.relay(dist, h, 1, held)
+
+            if held and h == 1:
+                @pl.when(inner & (dist == 1))
                 def _():
-                    self.along(z - dist, h, 0).start()
-                self.across(z - dist, h).start()
-                self.hand(z - dist, 0, h).start()
-
-            @pl.when(z + dist < 4)
-            def _():
-                self.along(z + dist, h, 1).wait_recv()
-
-                @pl.when(z > 0)
-                def _():
-                    self.along(z + dist, h, 1).start()
-                self.across(z + dist, h).start()
-                self.hand(z + dist, 0, h).start()
+                    for q in (0, 1):
+                        self.across(column(2), q).start()
 
         def relay_over(self, k, h):
             self.from_over(column(k), h).wait_recv()
@@ -250,7 +261,7 @@
         col = column(k)
         up = (col - z + 3) // 4
         dst, sem = rs_slot(1 - up, col, r, h)
-        return remote(hold.at[(k - 1) * 2 + r, pl.ds(h * QUARTER, QUARTER), :], dst,
+        return remote(hold.at[(k - 1) * 2 + r, pl.ds(pl.multiple_of(h * QUARTER, QUARTER), QUARTER), :], dst,
                       rss_sem.at[k - 1, r, h], sem, t - 4 + 8 * up)
 
     def take_sum(side, col, r, h, slot):
@@ -291,44 +302,19 @@
                     for h in (0, 1):
                         send_sum(k, q, h).start()
 
-    def hidden_step(n, carry):
-        k, h = n // 2, n % 2
-        gys.relay_row(k + 1, h)
-        gys.relay_over(k, h)
-
-        @pl.when(n > 0)
-        def _():
-            finish(n - 1)
-
-        @pl.when(inner & (n == 4))
-        def _():
-            xs.start_row()
-
-        @pl.when(n == 6)
-        def _():
-            xs.start_rest()
-            for q in (0, 1):
-                xs.relay_row(1, q)
-
-        gys.load(n, gy_b, gy_sem)
+    def hidden_step(n, buf, sem):
         for copy in load_u(n):
             copy.wait()
 
-        @pl.when(n == 0)
-        def _():
-            for copy in loads:
-                copy.wait()
-
         @pl.when(n > 0)
         def _():
             for copy in keep(n - 1):
                 copy.wait()
-            swap(n - 1).wait_send()
-        gys.landed(n, gy_b, gy_sem)
+        gys.landed(n, buf, sem)
 
         def hidden_tile(i, carry):
             at = pl.ds(pl.multiple_of(i * 256, 256), 256)
-            grad_h = dot_cols(wd_v[...], gy_b[at, :])
+            grad_h = dot_cols(wd_v[...], buf[at, :])
             gate = ug_b[:, at].astype(F32)
             up = uu_b[:, at].astype(F32)
             sig = jax.nn.sigmoid(gate)
@@ -350,6 +336,14 @@
             for copy in load_u(n + 1):
                 copy.start()
 
+        @pl.when((n > 0) & (n % 2 == 0))
+        def _():
+            finish(n - 1)
+
+        @pl.when(n > 0)
+        def _():
+            swap(n - 1).wait_send()
+
         def part_tile(j, carry):
             at = pl.ds(pl.multiple_of(j * 512, 512), 512)
             part = dot_plain(dgt_b[...], wg_v[:, at]) + dot_plain(dut_b[...], wu_v[:, at])
@@ -358,9 +352,60 @@
             return carry
         lax.fori_loop(0, hidden // 512, part_tile, 0)
         swap(n).start()
+
+    gys.load(0, gy_b, gy_sem)
+    for copy in loads:
+        copy.wait()
+    hidden_step(0, gy_b, gy_sem)
+
+    def hidden_pair(k, carry):
+        finish(2 * k)
+        for h in (0, 1):
+            gys.relay_row(k + 1, h, held=True)
+            gys.relay_over(k, h)
+
+            @pl.when(edge & (k == 3))
+            def _():
+                for side in (0, 1):
+                    @pl.when(z // 2 == 1 - side)
+                    def _():
+                        xs.relay(1, h, side)
+
+        gys.load(2 * k + 1, x_b, x_sem)
+
+        @pl.when(k < 3)
+        def _():
+            gys.load(2 * k + 2, gy_b, gy_sem)
+
+        @pl.when(inner & (k == 1))
+        def _():
+            xs.start_row()
+            xs.start_rest()
+            for side in (0, 1):
+                @pl.when(z == 1 + side)
+                def _():
+                    for h in (0, 1):
+                        xs.relay(1, h, side)
+
+        @pl.when(edge & (k == 2))
+        def _():
+            xs.start_rest()
+
+        @pl.when(inner & (k == 3))
+        def _():
+            for side in (0, 1):
+                @pl.when(z == 2 - side)
+                def _():
+                    for h in (0, 1):
+                        xs.relay(1, h, side)
+        hidden_step(2 * k + 1, x_b, x_sem)
+
+        @pl.when(k < 3)
+        def _():
+            hidden_step(2 * k + 2, gy_b, gy_sem)
         return carry
 
-    lax.fori_loop(0, CHIPS, hidden_step, 0)
+    lax.fori_loop(0, 4, hidden_pair, 0)
     finish(LAST)
     for copy in keep(LAST):
         copy.wait()
@@ -407,7 +452,7 @@
             lax.fori_loop(0, QUARTER // 32, tile, 0)
             give(h).start()
 
-    def weight_step(n, carry):
+    def weight_step(n):
         xs.load(n, x_b, x_sem)
         for i, c in ((0, core), (1, 1 - core)):
             @pl.when((n > 0) | (i == 1))
@@ -433,53 +478,45 @@
             acc_u[:, at] += dot_plain(du_b[...], x_b[:, at])
             return carry
         lax.fori_loop(0, hidden // 512, tile, 0)
-        return carry
 
     def late_step(i, carry):
-        for h in (0, 1):
-            xs.relay_row(i + 2, h)
-
         @pl.when(inner & (i == 0))
         def _():
             for r in (0, 1):
                 settle(z - 1, r)
-            carry_on(2, 0)
-            carry_on(2, 1)
-
-        @pl.when(inner & (i == 1))
-        def _():
-            carry_on(2, 2)
-            carry_on(2, 3)
-
-        @pl.when(inner & (i == 2))
-        def _():
-            carry_on(3, 0)
-        for h in (0, 1):
-            xs.relay_over(i, h)
-
-        @pl.when(inner & (i == 2))
-        def _():
-            settle(2 - z, 1)
-            give_over()
-            carry_on(3, 1)
-            carry_on(1, 0)
-            settle(2 - z, 0)
-        lax.fori_loop(2 * i, 2 * i + 2, weight_step, 0)
+
+        @pl.when(inner)
+        def _():
+            carry_on(2, i)
+
+        @pl.when(i < 2)
+        def _():
+            for h in (0, 1):
+                xs.relay_row(i + 2, h)
+        xs.relay_over(i // 2, i % 2)
+        weight_step(i)
         return carry
 
-    lax.fori_loop(0, 3, late_step, 0)
+    lax.fori_loop(0, 4, late_step, 0)
 
     @pl.when(inner)
     def _():
-        carry_on(3, 2)
-        carry_on(1, 1)
-    xs.relay_over(3, 0)
+        carry_on(3, 0)
+        settle(2 - z, 1)
+        give_over()
+        carry_on(3, 1)
+        carry_on(1, 0)
+        settle(2 - z, 0)
+    for h in (0, 1):
+        xs.relay_over(2, h)
 
     @pl.when(inner)
     def _():
-        carry_on(3, 3)
-        carry_on(1, 2)
-    xs.relay_over(3, 1)
+        for m in (1, 2):
+            carry_on(3, m + 1)
+            carry_on(1, m)
+    for h in (0, 1):
+        xs.relay_over(3, h)
 
     norm_loads = [pltpu.make_async_copy(src, x_b.at[pl.ds(k * own, own), :], x_sem.at[k])
                   for k, src in enumerate((xin, gres))]
@@ -549,7 +586,6 @@
             ds_next(1, d, h, mine).start()
             ds_twin(0, d, h, mine).start()
 
-    lax.fori_loop(6, 8, weight_step, 0)
     for d in (0, 1):
         gy_b[pl.ds(d * QUARTER, QUARTER), :] = out_ds[pl.ds(d * QUARTER, QUARTER), :]
 
@@ -586,6 +622,10 @@
     def ds_step(s, carry):
         ds_relay(s, 0)
         project(s - 1)
+
+        @pl.when(s < 5)
+        def _():
+            weight_step(s + 3)
         ds_relay(s, 1)
         for d in (0, 1):
             block_load(s, d, 0).start()

time: 367 us -> 325 us (0.89)
  Pallas kernels: 354 us -> 313 us
    pallas_call x1, Pallas kernels: 354 us -> 313 us  [local_backward(): pl.pallas_call(kernel, out_shape=[pltpu.VMEM((own, hidden), BF16), pltpu....]
where the time goes in v4:
time: 325 us; the launch traced here: 324 us
  Pallas kernels  313 us (96%)
  local copies, waits for them, and re-layouts  10.4 us (3%)
    pallas_call x1, Pallas kernels, local_backward(): pl.pallas_call(kernel, out_shape=[pltpu.VMEM((own, hidden), BF16), pltpu....  313 us
    unnamed x6, local copies, waits for them, and re-layouts  10.4 us

profile of v4, /device:TPU:0, one launch (start us, length us, event | category | flops | bytes accessed | tf_op | source)
XLA Modules:
  0.0 323.5 jit_solution(1324094727538702427)
XLA Ops:
  0.6 312.5 %mlp_backward.1 = (bf16[256,2048]{1,0:T(8,128)(2,1)S(1)}, bf16[4096,128]{1,0:T(8,128)(2,1)S(1)}, f32[688,2048]{1,0:T(8,128)S(1)}, f32[688,2048]{1,0:T(8,128)S(1)...) custom-call(bf16[256,2048]{1,0:T(8,128)(2,1)} %x.1, ...), custom_call_target="tpu_custom_call" | custom-call | tf_op jit(solution)/shard_map/mlp_backward/pallas_call | solution.py:680
  313.2 1.0 copy.24
  314.1 1.0 copy.25
  315.1 1.0 copy.29
  316.1 2.5 copy.26
  318.6 2.5 copy.27
  321.1 2.5 copy.28

commit v5 on v4

--- a/solution.py
+++ b/solution.py
@@ -15,6 +15,15 @@
 HALF = 64
 ROWS = 4 * QUARTER
 LAST = CHIPS - 1
+BOTH = (0, 1)
+TILE = 32
+WIDE = 512
+PART = 64
+PARTS = 2 * QUARTER // PART
+
+
+def tile_at(i, size, base=0):
+    return pl.ds(pl.multiple_of(base + i * size, size), size)
 
 
 def dot_cols(a, b):
@@ -156,7 +165,7 @@
             if held and h == 1:
                 @pl.when(inner & (dist == 1))
                 def _():
-                    for q in (0, 1):
+                    for q in BOTH:
                         self.across(column(2), q).start()
 
         def relay_over(self, k, h):
@@ -164,7 +173,7 @@
             self.hand(column(k), 1, h).start()
 
         def start_row(self):
-            for h in (0, 1):
+            for h in BOTH:
                 @pl.when(z < 3)
                 def _():
                     self.along(z, h, 0, self.mine(h)).start()
@@ -174,7 +183,7 @@
                     self.along(z, h, 1, self.mine(h)).start()
 
         def start_rest(self):
-            for h in (0, 1):
+            for h in BOTH:
                 self.across(z, h, self.mine(h)).start()
                 self.hand(z, 0, h, self.mine(h)).start()
 
@@ -188,7 +197,7 @@
             @pl.when(n > 0)
             def _():
                 self.block(n, core, buf, sem, 0).start()
-            for h in (0, 1):
+            for h in BOTH:
                 self.from_twin(column(k), r, h).wait_recv()
             self.block(n, 1 - core, buf, sem, 1).start()
 
@@ -197,13 +206,13 @@
             return pltpu.make_async_copy(self.full.at[rows, :], buf.at[pl.ds(i * own, own), :], sem.at[i])
 
         def landed(self, n, buf, sem):
-            for i in (0, 1):
+            for i in BOTH:
                 self.block(n, core, buf, sem, i).wait()
 
         def drain(self, col):
-            for h in (0, 1):
+            for h in BOTH:
                 self.across(col, h).wait_send()
-                for r in (0, 1):
+                for r in BOTH:
                     self.hand(col, r, h).wait_send()
 
                 @pl.when((z < 3) & (col <= z))
@@ -230,7 +239,7 @@
 
     def load_u(n):
         copies = []
-        for i in (0, 1):
+        for i in BOTH:
             c = core if i == 0 else 1 - core
             rows = pl.ds(first_row(column(n // 2), n % 2, c), own)
             at = pl.ds(i * own, own)
@@ -254,14 +263,14 @@
         return remote(p_send, p_recv.at[n % 2], ps_sem, pr_sem.at[n % 2], twin)
 
     def rs_slot(side, col, r, h):
-        rows = pl.multiple_of((((side * 4 + col) * 2 + line(r)) * 2 + h) * QUARTER, QUARTER)
-        return rs_in.at[pl.ds(rows, QUARTER), :], rsr_sem.at[side, col, line(r), h]
+        return (rs_in.at[tile_at(((side * 4 + col) * 2 + line(r)) * PARTS + h, PART), :],
+                rsr_sem.at[side, col, line(r), h])
 
     def send_sum(k, r, h):
         col = column(k)
         up = (col - z + 3) // 4
         dst, sem = rs_slot(1 - up, col, r, h)
-        return remote(hold.at[(k - 1) * 2 + r, pl.ds(pl.multiple_of(h * QUARTER, QUARTER), QUARTER), :], dst,
+        return remote(hold.at[(k - 1) * 2 + r, tile_at(h, PART), :], dst,
                       rss_sem.at[k - 1, r, h], sem, t - 4 + 8 * up)
 
     def take_sum(side, col, r, h, slot):
@@ -278,29 +287,29 @@
         @pl.when(k == 0)
         def _():
             def tile(i, carry):
-                at = pl.ds(pl.multiple_of(i * 32, 32), 32)
+                at = tile_at(i, TILE)
                 own_sum[r, at, :] = p_own[at, :] + p_recv[n % 2, at, :].astype(F32)
                 return carry
-            lax.fori_loop(0, own // 32, tile, 0)
+            lax.fori_loop(0, own // TILE, tile, 0)
 
         @pl.when(k > 0)
         def _():
             def tile(i, carry):
-                at = pl.ds(pl.multiple_of(i * 32, 32), 32)
+                at = tile_at(i, TILE)
                 hold[(k - 1) * 2 + r, at, :] = (p_own[at, :] + p_recv[n % 2, at, :].astype(F32)).astype(BF16)
                 return carry
-            lax.fori_loop(0, own // 32, tile, 0)
+            lax.fori_loop(0, own // TILE, tile, 0)
 
             @pl.when(edge & (k == 1))
             def _():
-                for h in (0, 1):
+                for h in range(PARTS):
                     send_sum(k, r, h).start()
 
             @pl.when(edge & (k > 1) & (r == 1))
             def _():
-                for q in (1, 0):
-                    for h in (0, 1):
-                        send_sum(k, q, h).start()
+                for q in BOTH:
+                    for h in range(PARTS):
+                        send_sum(k, 1 - q, h).start()
 
     def hidden_step(n, buf, sem):
         for copy in load_u(n):
@@ -345,12 +354,12 @@
             swap(n - 1).wait_send()
 
         def part_tile(j, carry):
-            at = pl.ds(pl.multiple_of(j * 512, 512), 512)
+            at = tile_at(j, WIDE)
             part = dot_plain(dgt_b[...], wg_v[:, at]) + dot_plain(dut_b[...], wu_v[:, at])
             p_own[:, at] = part[:own]
             p_send[:, at] = part[own:].astype(BF16)
             return carry
-        lax.fori_loop(0, hidden // 512, part_tile, 0)
+        lax.fori_loop(0, hidden // WIDE, part_tile, 0)
         swap(n).start()
 
     gys.load(0, gy_b, gy_sem)
@@ -360,13 +369,13 @@
 
     def hidden_pair(k, carry):
         finish(2 * k)
-        for h in (0, 1):
+        for h in BOTH:
             gys.relay_row(k + 1, h, held=True)
             gys.relay_over(k, h)
 
             @pl.when(edge & (k == 3))
             def _():
-                for side in (0, 1):
+                for side in BOTH:
                     @pl.when(z // 2 == 1 - side)
                     def _():
                         xs.relay(1, h, side)
@@ -381,10 +390,10 @@
         def _():
             xs.start_row()
             xs.start_rest()
-            for side in (0, 1):
+            for side in BOTH:
                 @pl.when(z == 1 + side)
                 def _():
-                    for h in (0, 1):
+                    for h in BOTH:
                         xs.relay(1, h, side)
 
         @pl.when(edge & (k == 2))
@@ -393,10 +402,10 @@
 
         @pl.when(inner & (k == 3))
         def _():
-            for side in (0, 1):
+            for side in BOTH:
                 @pl.when(z == 2 - side)
                 def _():
-                    for h in (0, 1):
+                    for h in BOTH:
                         xs.relay(1, h, side)
         hidden_step(2 * k + 1, x_b, x_sem)
 
@@ -412,39 +421,29 @@
     swap(LAST).wait_send()
 
     def carry_on(k, m):
-        r, h = 1 - m // 2, m % 2
+        r, h = 1 - m // PARTS, m % PARTS
         col = column(k)
         up = (col - z + 3) // 4
-        take_sum(1 - up, col, r, h, m % 2).wait()
-        base = h * QUARTER
-
-        def tile(i, carry):
-            at = pl.ds(pl.multiple_of(base + i * 32, 32), 32)
-            here = pl.ds(pl.multiple_of(i * 32, 32), 32)
-            total = hold[(k - 1) * 2 + r, at, :].astype(F32) + stage[m % 2, here, :].astype(F32)
-            hold[(k - 1) * 2 + r, at, :] = total.astype(BF16)
+        slot = m % 2
+        take_sum(1 - up, col, r, h, slot).wait()
+        mine = hold.at[(k - 1) * 2 + r, tile_at(h, PART), :]
+        mine[...] = (mine[...].astype(F32) + stage[slot].astype(F32)).astype(BF16)
+        send_sum(k, r, h).start()
+
+    def settle(side, r):
+        def part(h, carry):
+            take_sum(side, z, r, h, h % 2).wait()
+            at = tile_at(h, PART)
+            own_sum[r, at, :] = own_sum[r, at, :] + stage[h % 2].astype(F32)
             return carry
-        lax.fori_loop(0, QUARTER // 32, tile, 0)
-        send_sum(k, r, h).start()
-
-    def settle(side, r):
-        copies = [take_sum(side, z, r, h, h) for h in (0, 1)]
-        for h in (0, 1):
-            copies[h].wait()
-
-            def tile(i, carry):
-                at = pl.ds(pl.multiple_of(h * QUARTER + i * 32, 32), 32)
-                here = pl.ds(pl.multiple_of(i * 32, 32), 32)
-                own_sum[r, at, :] = own_sum[r, at, :] + stage[h, here, :].astype(F32)
-                return carry
-            lax.fori_loop(0, QUARTER // 32, tile, 0)
+        lax.fori_loop(0, PARTS, part, 0)
 
     def give(h):
         rows = pl.ds(h * QUARTER, QUARTER)
         return remote(p_send.at[rows, :], y_in.at[rows, :], yss_sem.at[h], ysr_sem.at[h], over)
 
     def give_over():
-        for h in (0, 1):
+        for h in BOTH:
             def tile(i, carry):
                 at = pl.ds(pl.multiple_of(h * QUARTER + i * 32, 32), 32)
                 p_send[at, :] = own_sum[1, at, :].astype(BF16)
@@ -472,32 +471,47 @@
         xs.landed(n, x_b, x_sem)
 
         def tile(j, carry):
-            at = pl.ds(pl.multiple_of(j * 512, 512), 512)
+            at = tile_at(j, WIDE)
             acc_d[:, at] += dot_plain(z_b[...], gy_b[:, at])
+            return carry
+        lax.fori_loop(0, hidden // WIDE, tile, 0)
+
+    def weight_rest():
+        def tile(j, carry):
+            at = tile_at(j, WIDE)
             acc_g[:, at] += dot_plain(dg_b[...], x_b[:, at])
             acc_u[:, at] += dot_plain(du_b[...], x_b[:, at])
             return carry
-        lax.fori_loop(0, hidden // 512, tile, 0)
+        lax.fori_loop(0, hidden // WIDE, tile, 0)
 
     def late_step(i, carry):
-        @pl.when(inner & (i == 0))
-        def _():
-            for r in (0, 1):
-                settle(z - 1, r)
-
         @pl.when(inner)
         def _():
-            carry_on(2, i)
+            carry_on(2, 2 * i)
+            carry_on(2, 2 * i + 1)
 
         @pl.when(i < 2)
         def _():
-            for h in (0, 1):
+            for h in BOTH:
                 xs.relay_row(i + 2, h)
         xs.relay_over(i // 2, i % 2)
-        weight_step(i)
+
+        @pl.when(i < 2)
+        def _():
+            weight_step(i)
+            weight_rest()
+
+        @pl.when(inner & (i > 1))
+        def _():
+            settle(z - 1, i - 2)
         return carry
 
     lax.fori_loop(0, 4, late_step, 0)
+
+    def pass_two(m, carry):
+        carry_on(3, m)
+        carry_on(1, m - 2)
+        return carry
 
     @pl.when(inner)
     def _():
@@ -505,17 +519,15 @@
         settle(2 - z, 1)
         give_over()
         carry_on(3, 1)
-        carry_on(1, 0)
+        lax.fori_loop(2, PARTS, pass_two, 0)
         settle(2 - z, 0)
-    for h in (0, 1):
+    for h in BOTH:
         xs.relay_over(2, h)
 
     @pl.when(inner)
     def _():
-        for m in (1, 2):
-            carry_on(3, m + 1)
-            carry_on(1, m)
-    for h in (0, 1):
+        lax.fori_loop(PARTS, 2 * PARTS, pass_two, 0)
+    for h in BOTH:
         xs.relay_over(3, h)
 
     norm_loads = [pltpu.make_async_copy(src, x_b.at[pl.ds(k * own, own), :], x_sem.at[k])
@@ -525,7 +537,8 @@
 
     @pl.when(inner)
     def _():
-        carry_on(1, 3)
+        carry_on(1, 2 * PARTS - 2)
+        carry_on(1, 2 * PARTS - 1)
 
     @pl.when(edge)
     def _():
@@ -565,10 +578,10 @@
                       ds_ps.at[s, 2 * d + h], ds_pr.at[s, 2 * d + h], twin)
 
     gain = gamma[...].astype(F32)[None, :]
-    for d in (0, 1):
+    for d in BOTH:
         give(d).wait_recv()
-    for h in (0, 1):
-        for d in (0, 1):
+    for h in BOTH:
+        for d in BOTH:
             def norm_tile(i, carry):
                 here = pl.ds(pl.multiple_of(d * QUARTER + h * HALF + i * 16, 16), 16)
                 skip = pl.ds(pl.multiple_of(2 * QUARTER + d * QUARTER + h * HALF + i * 16, 16), 16)
@@ -586,32 +599,32 @@
             ds_next(1, d, h, mine).start()
             ds_twin(0, d, h, mine).start()
 
-    for d in (0, 1):
+    for d in BOTH:
         gy_b[pl.ds(d * QUARTER, QUARTER), :] = out_ds[pl.ds(d * QUARTER, QUARTER), :]
 
     def project(s):
-        for d in (0, 1):
-            for h in (0, 1):
+        for d in BOTH:
+            for h in BOTH:
                 ds_from_twin(s, d, h).wait_recv()
             block_load(s, d, 1).start()
-        for d in (0, 1):
+        for d in BOTH:
             block_load(s, d, 1).wait()
-        for k in (0, 1):
-            for d in (0, 1):
+        for k in BOTH:
+            for d in BOTH:
                 c = core if k == 0 else 1 - core
                 rows = pl.ds(row(s, d, c), QUARTER)
                 at = pl.ds((2 * k + d) * QUARTER, QUARTER)
                 z_b[pl.ds(0, QUARTER), at] = att_v[rows, :].T
         grad_o = dot_cols(gy_b[...], wo_v[...]).astype(BF16)
-        for k in (0, 1):
-            for d in (0, 1):
+        for k in BOTH:
+            for d in BOTH:
                 c = core if k == 0 else 1 - core
                 do_v[pl.ds(row(s, d, c), QUARTER), :] = grad_o[(2 * k + d) * QUARTER:(2 * k + d + 1) * QUARTER]
-        for j in range(0, hidden, 512):
-            acc_o[:, j:j + 512] += dot_plain(z_b[pl.ds(0, QUARTER), :], gy_b[:, j:j + 512])
+        for j in range(0, hidden, WIDE):
+            acc_o[:, j:j + WIDE] += dot_plain(z_b[:QUARTER, :], gy_b[:, j:j + WIDE])
 
     def ds_relay(s, h):
-        for d in (0, 1):
+        for d in BOTH:
             ds_here(s, d, h).wait_recv()
 
             @pl.when(s < LAST)
@@ -623,13 +636,17 @@
         ds_relay(s, 0)
         project(s - 1)
 
-        @pl.when(s < 5)
-        def _():
-            weight_step(s + 3)
+        @pl.when(s < LAST)
+        def _():
+            weight_step(s + 1)
         ds_relay(s, 1)
-        for d in (0, 1):
+        for d in BOTH:
             block_load(s, d, 0).start()
-        for d in (0, 1):
+
+        @pl.when(s < LAST)
+        def _():
+            weight_rest()
+        for d in BOTH:
             block_load(s, d, 0).wait()
         return carry
 
@@ -637,13 +654,13 @@
     project(LAST)
 
     def drain(s, carry):
-        for d in (0, 1):
-            for h in (0, 1):
+        for d in BOTH:
+            for h in BOTH:
                 ds_twin(s, d, h).wait_send()
 
             @pl.when(s > 0)
             def _():
-                for h in (0, 1):
+                for h in BOTH:
                     ds_here(s, d, h).wait_send()
         return carry
     lax.fori_loop(0, CHIPS, drain, 0)
@@ -654,13 +671,22 @@
 
         @pl.when(col > 0)
         def _():
-            for r in (0, 1):
-                for h in (0, 1):
+            for r in BOTH:
+                for h in range(PARTS):
                     send_sum(col, r, h).wait_send()
         return carry
     lax.fori_loop(0, 4, drain_columns, 0)
-    for h in (0, 1):
+    for h in BOTH:
         give(h).wait_send()
+
+
+def write_out(*refs):
+    count = len(refs) // 2
+    copies = [pltpu.make_async_copy(refs[i], refs[count + i], refs[-1].at[i]) for i in range(count)]
+    for copy in copies:
+        copy.start()
+    for copy in copies:
+        copy.wait()
 
 
 def solution(mesh):
@@ -677,6 +703,8 @@
         inside = pl.BlockSpec(memory_space=pltpu.VMEM)
         shape = jax.ShapeDtypeStruct
         dma = pltpu.SemaphoreType.DMA
+        pair = (2,)
+        stream_sems = [dma((2, 4, 2))] + [dma((4, 2))] * 3 + [dma((2, 4, 2))] * 2
         outs = pl.pallas_call(
             kernel,
             out_shape=[
@@ -684,7 +712,7 @@
                 pltpu.VMEM((ffn, hidden), F32), pltpu.VMEM((ffn, hidden), F32), pltpu.VMEM((ffn, hidden), F32),
                 pltpu.VMEM((cols, hidden), F32),
                 shape((tokens, hidden), BF16), shape((tokens, hidden), BF16), shape((tokens, hidden), BF16),
-                shape((32 * QUARTER, hidden), BF16),
+                shape((tokens, hidden), BF16),
                 shape((CHIPS, ffn, ROWS), BF16), shape((CHIPS, ffn, ROWS), BF16), shape((CHIPS, ffn, ROWS), BF16),
             ],
             in_specs=[anywhere] * 8 + [inside] + [anywhere] * 3,
@@ -697,19 +725,28 @@
                 pltpu.VMEM((ROWS, ffn), BF16), pltpu.VMEM((ROWS, ffn), BF16),
                 pltpu.VMEM((own, hidden), F32), pltpu.VMEM((own, hidden), BF16), pltpu.VMEM((2, own, hidden), BF16),
                 pltpu.VMEM((6, own, hidden), BF16), pltpu.VMEM((2, own, hidden), F32),
-                pltpu.VMEM((2, QUARTER, hidden), BF16), pltpu.VMEM((own, hidden), BF16),
+                pltpu.VMEM((2, PART, hidden), BF16), pltpu.VMEM((own, hidden), BF16),
                 pltpu.VMEM((tokens, cols), BF16), pltpu.VMEM((cols, hidden), BF16),
-                dma((2, 4, 2)), dma((4, 2)), dma((4, 2)), dma((4, 2)), dma((2, 4, 2)), dma((2, 4, 2)),
-                dma((2, 4, 2)), dma((4, 2)), dma((4, 2)), dma((4, 2)), dma((2, 4, 2)), dma((2, 4, 2)),
-                dma((CHIPS, 4)), dma((CHIPS, 4)), dma((CHIPS, 4)), dma((CHIPS, 4)),
-                dma, dma((2,)), dma((3, 2, 2)), dma((2, 4, 2, 2)), dma((2,)), dma((2,)),
-                dma((5,)), dma((4,)), dma((2,)), dma((4,)), dma((3,)), dma((2,)),
+                *stream_sems,
+                *stream_sems,
+                *[dma((CHIPS, 4))] * 4,
+                dma, dma(pair), dma((3, 2, PARTS)), dma((2, 4, 2, PARTS)), dma(pair), dma(pair),
+                dma((5,)), dma((4,)), dma(pair), dma((4,)), dma((3,)), dma(pair),
             ],
             compiler_params=pltpu.CompilerParams(
                 collective_id=0, has_side_effects=True, vmem_limit_bytes=44 * 2 ** 20),
             name="mlp_backward",
         )(x_norm, grad_y, u_gate.T, u_up.T, w_gate.T, w_up.T, w_down, x_in, gamma, grad_res, attn_out, w_out)
-        grad_sum, grad_attn, gw_gate, gw_up, gw_down, gw_out = outs[:6]
+        results = outs[:6]
+        grad_sum, grad_attn, gw_gate, gw_up, gw_down, gw_out = pl.pallas_call(
+            write_out,
+            out_shape=[shape(a.shape, a.dtype) for a in results],
+            in_specs=[inside] * len(results),
+            out_specs=[anywhere] * len(results),
+            scratch_shapes=[dma((len(results),))],
+            compiler_params=pltpu.CompilerParams(vmem_limit_bytes=2 ** 20),
+            name="write_out",
+        )(*results)
         return grad_sum, grad_attn, gw_gate.T, gw_up.T, gw_down, gw_out
 
     return jax.shard_map(

time: 325 us -> 312 us (0.960)
  local copies, waits for them, and re-layouts: 10.4 us -> 0 us
  Pallas kernels: 313 us -> 309 us
    pallas_call x1, Pallas kernels: 313 us -> 302 us  [local_backward(): pl.pallas_call(kernel, out_shape=[pltpu.VMEM((own, hidden), BF16), pltpu....]
    unnamed x6 -> x0, local copies, waits for them, and re-layouts: 10.4 us -> none
    pallas_call x0 -> x1, Pallas kernels: none -> 6.96 us  [local_backward(): pl.pallas_call(write_out, out_shape=[shape(a.shape, a.dtype) for a in res...]
where the time goes in v5:
time: 312 us; the launch traced here: 310 us
  Pallas kernels  309 us (99%)
    pallas_call x1, Pallas kernels, local_backward(): pl.pallas_call(kernel, out_shape=[pltpu.VMEM((own, hidden), BF16), pltpu....  302 us
    pallas_call x1, Pallas kernels, local_backward(): pl.pallas_call(write_out, out_shape=[shape(a.shape, a.dtype) for a in res...  6.96 us

profile of v5, /device:TPU:0, one launch (start us, length us, event | category | flops | bytes accessed | tf_op | source)
XLA Modules:
  0.0 309.8 jit_solution(2085331625451507028)
XLA Ops:
  0.6 302.1 %mlp_backward.1 = (bf16[256,2048]{1,0:T(8,128)(2,1)S(1)}, bf16[4096,128]{1,0:T(8,128)(2,1)S(1)}, f32[688,2048]{1,0:T(8,128)S(1)}, f32[688,2048]{1,0:T(8,128)S(1)...) custom-call(bf16[256,2048]{1,0:T(8,128)(2,1)} %x.1, ...), custom_call_target="tpu_custom_call" | custom-call | tf_op jit(solution)/shard_map/mlp_backward/pallas_call | solution.py:708
  302.7 7.0 %write_out.1 = (bf16[256,2048]{1,0:T(8,128)(2,1)}, bf16[4096,128]{1,0:T(8,128)(2,1)}, f32[688,2048]{1,0:T(8,128)}, f32[688,2048]{1,0:T(8,128)}, f32[688,2048]{1,0:T(8,128)}, /*index=5*/f32[128,2048]{1,0:T(8,128)}) custom-call(bf16[256,2048]{1,0:T(8,128)(2,1)S(1)} %get-tuple-element.18.refs_0_, bf16[4096,128]{1,0:T(8,128)(2,1)S(1)} %get-tuple-element.19.refs_1_, ...), custom_call_target="tpu_custom_call" | custom-call | tf_op jit(solution)/shard_map/write_out/pallas_call | solution.py:741

commit v6 on v5

--- a/solution.py
+++ b/solution.py
@@ -20,6 +20,7 @@
 WIDE = 512
 PART = 64
 PARTS = 2 * QUARTER // PART
+SPARE = 64
 
 
 def tile_at(i, size, base=0):
@@ -40,7 +41,7 @@
            gy_b, x_b, ug_b, uu_b, z_b, dg_b, du_b, dgt_b, dut_b,
            p_own, p_send, p_recv, hold, own_sum, stage, y_in,
            att_v, wo_v,
-           gy_zs, gy_zr, gy_ys, gy_yr, gy_ts, gy_tr, x_zs, x_zr, x_ys, x_yr, x_ts, x_tr,
+           gy_zs, gy_zr, gy_ys, gy_yr, gy_ts, gy_tr, x_zs, x_zr, x_ys, x_yr, x_ts, x_tr, e_zs, e_zr, e_ts, e_tr,
            ds_ss, ds_rs, ds_ps, ds_pr, ps_sem, pr_sem, rss_sem, rsr_sem, yss_sem, ysr_sem,
            w_sem, gy_sem, x_sem, u_sem, keep_sem, stage_sem):
     hidden = gy.shape[1]
@@ -106,12 +107,55 @@
         return pl.ds(pl.multiple_of(first_row(col, r, c) + h * QUARTER, QUARTER), QUARTER)
 
     class Stream:
-        def __init__(self, own_ref, full, zs, zr, ys, yr, ts, tr):
+        def __init__(self, own_ref, full, zs, zr, ys, yr, ts, tr, spare=None):
             self.own, self.full = own_ref, full
+            self.spare = spare
             self.zs, self.zr, self.ys, self.yr, self.ts, self.tr = zs, zr, ys, yr, ts, tr
 
-        def part(self, col, r, c, h):
+        def part(self, col, r, c, h, short=False):
+            if short and self.spare is not None and h == 1:
+                start = pl.multiple_of(first_row(col, r, c) + QUARTER, QUARTER)
+                return self.full.at[pl.ds(start, QUARTER - SPARE), :]
             return self.full.at[half(col, r, c, h), :]
+
+        def either(self, col, h, act):
+            if self.spare is None or h == 0:
+                act(False)
+                return
+            thin = (col % 3 != 0) & (col != z)
+            pl.when(thin)(lambda: act(True))
+            pl.when(jnp.logical_not(thin))(lambda: act(False))
+
+        def spare_part(self, col, c):
+            start = pl.multiple_of(first_row(col, 1, c) + 2 * QUARTER - SPARE, 16)
+            return self.full.at[pl.ds(start, SPARE), :]
+
+        def spare_along(self, col, side):
+            dst = self.spare_part(col, core)
+            return remote(dst, dst, self.spare[0].at[side, col], self.spare[1].at[col], beside[side])
+
+        def spare_hand(self, col, c):
+            dst = self.spare_part(col, c)
+            return remote(dst, dst, self.spare[2].at[col], self.spare[3].at[col], twin)
+
+        def spare_start(self):
+            @pl.when(inner)
+            def _():
+                for side in BOTH:
+                    self.spare_along(z, side).start()
+
+        def spare_relay(self, dist):
+            for side in BOTH:
+                col = z - dist if side == 0 else z + dist
+
+                @pl.when((col == 1) | (col == 2))
+                def _():
+                    self.spare_along(col, side).wait_recv()
+
+                    @pl.when(z < 3 if side == 0 else z > 0)
+                    def _():
+                        self.spare_along(col, side).start()
+                    self.spare_hand(col, core).start()
 
         def mine(self, h):
             return self.own.at[pl.ds(h * QUARTER, QUARTER), :]
@@ -120,20 +164,20 @@
             dst = self.part(col, 0, core, h)
             return remote(dst if src is None else src, dst, self.zs.at[side, col, h], self.zr.at[col, h], beside[side])
 
-        def across(self, col, h, src=None):
-            dst = self.part(col, 0, core, h)
+        def across(self, col, h, src=None, short=False):
+            dst = self.part(col, 0, core, h, short)
             return remote(dst if src is None else src, dst, self.ys.at[col, h], self.yr.at[col, h], over)
 
-        def from_over(self, col, h):
-            dst = self.part(col, 1, core, h)
+        def from_over(self, col, h, short):
+            dst = self.part(col, 1, core, h, short)
             return remote(dst, dst, self.ys.at[col, h], self.yr.at[col, h], over)
 
-        def hand(self, col, r, h, src=None):
-            dst = self.part(col, r, core, h)
+        def hand(self, col, r, h, src=None, short=False):
+            dst = self.part(col, r, core, h, short)
             return remote(dst if src is None else src, dst, self.ts.at[r, col, h], self.tr.at[r, col, h], twin)
 
-        def from_twin(self, col, r, h):
-            dst = self.part(col, r, 1 - core, h)
+        def from_twin(self, col, r, h, short=False):
+            dst = self.part(col, r, 1 - core, h, short)
             return remote(dst, dst, self.ts.at[r, col, h], self.tr.at[r, col, h], twin)
 
         def relay(self, dist, h, side, held=False):
@@ -145,7 +189,7 @@
                 self.along(col, h, side).start()
             self.hand(col, 0, h).start()
             if not held:
-                self.across(col, h).start()
+                self.either(col, h, lambda short: self.across(col, h, short=short).start())
             else:
                 second = inner & (dist == 1) & (z == 2 - side)
 
@@ -169,8 +213,12 @@
                         self.across(column(2), q).start()
 
         def relay_over(self, k, h):
-            self.from_over(column(k), h).wait_recv()
-            self.hand(column(k), 1, h).start()
+            col = column(k)
+
+            def act(short):
+                self.from_over(col, h, short).wait_recv()
+                self.hand(col, 1, h, short=short).start()
+            self.either(col, h, act)
 
         def start_row(self):
             for h in BOTH:
@@ -197,8 +245,21 @@
             @pl.when(n > 0)
             def _():
                 self.block(n, core, buf, sem, 0).start()
-            for h in BOTH:
-                self.from_twin(column(k), r, h).wait_recv()
+            if self.spare is None:
+                for h in BOTH:
+                    self.from_twin(column(k), r, h).wait_recv()
+            else:
+                cut = (k > 0) & (r == 1) & (column(k) % 3 != 0)
+                self.from_twin(column(k), r, 0).wait_recv()
+
+                @pl.when(cut)
+                def _():
+                    self.from_twin(column(k), r, 1, True).wait_recv()
+                    self.spare_hand(column(k), 1 - core).wait_recv()
+
+                @pl.when(jnp.logical_not(cut))
+                def _():
+                    self.from_twin(column(k), r, 1).wait_recv()
             self.block(n, 1 - core, buf, sem, 1).start()
 
         def block(self, n, c, buf, sem, i):
@@ -211,20 +272,26 @@
 
         def drain(self, col):
             for h in BOTH:
-                self.across(col, h).wait_send()
-                for r in BOTH:
-                    self.hand(col, r, h).wait_send()
-
-                @pl.when((z < 3) & (col <= z))
-                def _():
-                    self.along(col, h, 0).wait_send()
-
-                @pl.when((z > 0) & (col >= z))
-                def _():
-                    self.along(col, h, 1).wait_send()
+                self.hand(col, 0, h).wait_send()
+
+                def act(short):
+                    self.across(col, h, short=short).wait_send()
+                    self.hand(col, 1, h, short=short).wait_send()
+                    if short:
+                        self.spare_hand(col, core).wait_send()
+                self.either(col, h, act)
+            for side in BOTH:
+                @pl.when((z < 3) & (col <= z) if side == 0 else (z > 0) & (col >= z))
+                def _():
+                    for h in BOTH:
+                        self.along(col, h, side).wait_send()
+                    if self.spare is not None:
+                        @pl.when(col % 3 != 0)
+                        def _():
+                            self.spare_along(col, side).wait_send()
 
     gys = Stream(gy, gy_all, gy_zs, gy_zr, gy_ys, gy_yr, gy_ts, gy_tr)
-    xs = Stream(x, x_all, x_zs, x_zr, x_ys, x_yr, x_ts, x_tr)
+    xs = Stream(x, x_all, x_zs, x_zr, x_ys, x_yr, x_ts, x_tr, (e_zs, e_zr, e_ts, e_tr))
     gys.start_row()
     gys.start_rest()
 
@@ -307,9 +374,13 @@
 
             @pl.when(edge & (k > 1) & (r == 1))
             def _():
-                for q in BOTH:
-                    for h in range(PARTS):
-                        send_sum(k, 1 - q, h).start()
+                for h in range(PARTS):
+                    send_sum(k, 1, h).start()
+
+            @pl.when(edge & (k == 3) & (r == 1))
+            def _():
+                for h in range(PARTS):
+                    send_sum(3, 0, h).start()
 
     def hidden_step(n, buf, sem):
         for copy in load_u(n):
@@ -380,12 +451,6 @@
                     def _():
                         xs.relay(1, h, side)
 
-        gys.load(2 * k + 1, x_b, x_sem)
-
-        @pl.when(k < 3)
-        def _():
-            gys.load(2 * k + 2, gy_b, gy_sem)
-
         @pl.when(inner & (k == 1))
         def _():
             xs.start_row()
@@ -395,6 +460,12 @@
                 def _():
                     for h in BOTH:
                         xs.relay(1, h, side)
+
+        gys.load(2 * k + 1, x_b, x_sem)
+
+        @pl.when(k < 3)
+        def _():
+            gys.load(2 * k + 2, gy_b, gy_sem)
 
         @pl.when(edge & (k == 2))
         def _():
@@ -485,16 +556,36 @@
         lax.fori_loop(0, hidden // WIDE, tile, 0)
 
     def late_step(i, carry):
-        @pl.when(inner)
+        @pl.when(inner & (i < 2))
         def _():
             carry_on(2, 2 * i)
             carry_on(2, 2 * i + 1)
 
+        @pl.when(inner & (i > 1))
+        def _():
+            carry_on(3, 2 * i - 4)
+            carry_on(3, 2 * i - 3)
+
         @pl.when(i < 2)
         def _():
             for h in BOTH:
                 xs.relay_row(i + 2, h)
-        xs.relay_over(i // 2, i % 2)
+
+        for h in BOTH:
+            @pl.when(i == h)
+            def _():
+                xs.relay_over(0, h)
+                if h == 1:
+                    xs.spare_start()
+
+                    @pl.when(edge)
+                    def _():
+                        for q in range(PARTS):
+                            send_sum(2, 0, q).start()
+
+            @pl.when(i == 2 + h)
+            def _():
+                xs.relay_over(1, h)
 
         @pl.when(i < 2)
         def _():
@@ -508,25 +599,33 @@
 
     lax.fori_loop(0, 4, late_step, 0)
 
-    def pass_two(m, carry):
-        carry_on(3, m)
-        carry_on(1, m - 2)
-        return carry
-
     @pl.when(inner)
     def _():
-        carry_on(3, 0)
         settle(2 - z, 1)
         give_over()
-        carry_on(3, 1)
-        lax.fori_loop(2, PARTS, pass_two, 0)
-        settle(2 - z, 0)
+
+        def both_ways(m, carry):
+            carry_on(1, m)
+            carry_on(3, m + PARTS)
+            return carry
+        lax.fori_loop(0, PARTS, both_ways, 0)
     for h in BOTH:
         xs.relay_over(2, h)
 
+    @pl.when(edge)
+    def _():
+        settle((3 - z) // 3, 1)
+        give_over()
+    xs.spare_relay(1)
+
     @pl.when(inner)
     def _():
-        lax.fori_loop(PARTS, 2 * PARTS, pass_two, 0)
+        def both_ways(m, carry):
+            carry_on(1, m)
+            carry_on(2, m)
+            return carry
+        lax.fori_loop(PARTS, 2 * PARTS, both_ways, 0)
+    xs.spare_relay(2)
     for h in BOTH:
         xs.relay_over(3, h)
 
@@ -537,13 +636,10 @@
 
     @pl.when(inner)
     def _():
-        carry_on(1, 2 * PARTS - 2)
-        carry_on(1, 2 * PARTS - 1)
+        settle(2 - z, 0)
 
     @pl.when(edge)
     def _():
-        settle((3 - z) // 3, 1)
-        give_over()
         settle((3 - z) // 3, 0)
     for copy in norm_loads:
         copy.wait()
@@ -728,7 +824,7 @@
                 pltpu.VMEM((2, PART, hidden), BF16), pltpu.VMEM((own, hidden), BF16),
                 pltpu.VMEM((tokens, cols), BF16), pltpu.VMEM((cols, hidden), BF16),
                 *stream_sems,
-                *stream_sems,
+                *stream_sems, dma((2, 4)), *[dma((4,))] * 3,
                 *[dma((CHIPS, 4))] * 4,
                 dma, dma(pair), dma((3, 2, PARTS)), dma((2, 4, 2, PARTS)), dma(pair), dma(pair),
                 dma((5,)), dma((4,)), dma(pair), dma((4,)), dma((3,)), dma(pair),

time: 312 us -> 307 us (0.984)
  Pallas kernels: 309 us -> 305 us
    pallas_call x1, Pallas kernels: 302 us -> 298 us  [local_backward(): pl.pallas_call(kernel, out_shape=[pltpu.VMEM((own, hidden), BF16), pltpu....]
where the time goes in v6:
time: 307 us; the launch traced here: 306 us
  Pallas kernels  305 us (99%)
    pallas_call x1, Pallas kernels, local_backward(): pl.pallas_call(kernel, out_shape=[pltpu.VMEM((own, hidden), BF16), pltpu....  298 us
    pallas_call x1, Pallas kernels, local_backward(): pl.pallas_call(write_out, out_shape=[shape(a.shape, a.dtype) for a in res...  6.96 us

profile of v6, /device:TPU:0, one launch (start us, length us, event | category | flops | bytes accessed | tf_op | source)
XLA Modules:
  0.0 305.7 jit_solution(5959096570186145149)
XLA Ops:
  0.6 298.0 %mlp_backward.1 = (bf16[256,2048]{1,0:T(8,128)(2,1)S(1)}, bf16[4096,128]{1,0:T(8,128)(2,1)S(1)}, f32[688,2048]{1,0:T(8,128)S(1)}, f32[688,2048]{1,0:T(8,128)S(1)...) custom-call(bf16[256,2048]{1,0:T(8,128)(2,1)} %x.1, ...), custom_call_target="tpu_custom_call" | custom-call | tf_op jit(solution)/shard_map/mlp_backward/pallas_call | solution.py:804
  298.6 7.0 %write_out.1 = (bf16[256,2048]{1,0:T(8,128)(2,1)}, bf16[4096,128]{1,0:T(8,128)(2,1)}, f32[688,2048]{1,0:T(8,128)}, f32[688,2048]{1,0:T(8,128)}, f32[688,2048]{1,0:T(8,128)}, /*index=5*/f32[128,2048]{1,0:T(8,128)}) custom-call(bf16[256,2048]{1,0:T(8,128)(2,1)S(1)} %get-tuple-element.18.refs_0_, bf16[4096,128]{1,0:T(8,128)(2,1)S(1)} %get-tuple-element.19.refs_1_, ...), custom_call_target="tpu_custom_call" | custom-call | tf_op jit(solution)/shard_map/write_out/pallas_call | solution.py:837

commit v7 on v6

--- a/solution.py
+++ b/solution.py
@@ -21,6 +21,10 @@
 PART = 64
 PARTS = 2 * QUARTER // PART
 SPARE = 64
+
+
+def part_of(q):
+    return 2 * (q % 2) + q // 2
 
 
 def tile_at(i, size, base=0):
@@ -369,18 +373,18 @@
 
             @pl.when(edge & (k == 1))
             def _():
-                for h in range(PARTS):
-                    send_sum(k, r, h).start()
+                for q in range(PARTS):
+                    send_sum(k, r, part_of(q)).start()
 
             @pl.when(edge & (k > 1) & (r == 1))
             def _():
-                for h in range(PARTS):
-                    send_sum(k, 1, h).start()
+                for q in range(PARTS):
+                    send_sum(k, 1, part_of(q)).start()
 
             @pl.when(edge & (k == 3) & (r == 1))
             def _():
-                for h in range(PARTS):
-                    send_sum(3, 0, h).start()
+                for q in range(PARTS):
+                    send_sum(3, 0, part_of(q)).start()
 
     def hidden_step(n, buf, sem):
         for copy in load_u(n):
@@ -492,7 +496,7 @@
     swap(LAST).wait_send()
 
     def carry_on(k, m):
-        r, h = 1 - m // PARTS, m % PARTS
+        r, h = 1 - m // PARTS, part_of(m % PARTS)
         col = column(k)
         up = (col - z + 3) // 4
         slot = m % 2
@@ -501,26 +505,26 @@
         mine[...] = (mine[...].astype(F32) + stage[slot].astype(F32)).astype(BF16)
         send_sum(k, r, h).start()
 
+    def settle_part(side, r, h, slot):
+        take_sum(side, z, r, h, slot).wait()
+        at = tile_at(h, PART)
+        own_sum[r, at, :] = own_sum[r, at, :] + stage[slot].astype(F32)
+
     def settle(side, r):
-        def part(h, carry):
-            take_sum(side, z, r, h, h % 2).wait()
-            at = tile_at(h, PART)
-            own_sum[r, at, :] = own_sum[r, at, :] + stage[h % 2].astype(F32)
+        def part(q, carry):
+            settle_part(side, r, part_of(q), q % 2)
             return carry
         lax.fori_loop(0, PARTS, part, 0)
 
     def give(h):
-        rows = pl.ds(h * QUARTER, QUARTER)
+        rows = pl.ds(h * PART, PART)
         return remote(p_send.at[rows, :], y_in.at[rows, :], yss_sem.at[h], ysr_sem.at[h], over)
 
     def give_over():
-        for h in BOTH:
-            def tile(i, carry):
-                at = pl.ds(pl.multiple_of(h * QUARTER + i * 32, 32), 32)
-                p_send[at, :] = own_sum[1, at, :].astype(BF16)
-                return carry
-            lax.fori_loop(0, QUARTER // 32, tile, 0)
-            give(h).start()
+        for q in range(PARTS):
+            rows = pl.ds(part_of(q) * PART, PART)
+            p_send[rows, :] = own_sum[1, rows, :].astype(BF16)
+            give(part_of(q)).start()
 
     def weight_step(n):
         xs.load(n, x_b, x_sem)
@@ -581,7 +585,7 @@
                     @pl.when(edge)
                     def _():
                         for q in range(PARTS):
-                            send_sum(2, 0, q).start()
+                            send_sum(2, 0, part_of(q)).start()
 
             @pl.when(i == 2 + h)
             def _():
@@ -634,13 +638,6 @@
     for copy in norm_loads:
         copy.start()
 
-    @pl.when(inner)
-    def _():
-        settle(2 - z, 0)
-
-    @pl.when(edge)
-    def _():
-        settle((3 - z) // 3, 0)
     for copy in norm_loads:
         copy.wait()
 
@@ -674,10 +671,11 @@
                       ds_ps.at[s, 2 * d + h], ds_pr.at[s, 2 * d + h], twin)
 
     gain = gamma[...].astype(F32)[None, :]
-    for d in BOTH:
-        give(d).wait_recv()
     for h in BOTH:
         for d in BOTH:
+            settle_part((3 - z) // 2, 0, 2 * d + h, d)
+            give(2 * d + h).wait_recv()
+
             def norm_tile(i, carry):
                 here = pl.ds(pl.multiple_of(d * QUARTER + h * HALF + i * 16, 16), 16)
                 skip = pl.ds(pl.multiple_of(2 * QUARTER + d * QUARTER + h * HALF + i * 16, 16), 16)
@@ -728,6 +726,17 @@
                 ds_next(s + 1, d, h).start()
             ds_twin(s, d, h).start()
 
+    def drain_columns(col, carry):
+        gys.drain(col)
+        xs.drain(col)
+
+        @pl.when(col > 0)
+        def _():
+            for r in BOTH:
+                for h in range(PARTS):
+                    send_sum(col, r, h).wait_send()
+        return carry
+
     def ds_step(s, carry):
         ds_relay(s, 0)
         project(s - 1)
@@ -735,6 +744,12 @@
         @pl.when(s < LAST)
         def _():
             weight_step(s + 1)
+
+        @pl.when(s == LAST)
+        def _():
+            lax.fori_loop(0, 4, drain_columns, 0)
+            for q in range(PARTS):
+                give(q).wait_send()
         ds_relay(s, 1)
         for d in BOTH:
             block_load(s, d, 0).start()
@@ -760,20 +775,6 @@
                     ds_here(s, d, h).wait_send()
         return carry
     lax.fori_loop(0, CHIPS, drain, 0)
-
-    def drain_columns(col, carry):
-        gys.drain(col)
-        xs.drain(col)
-
-        @pl.when(col > 0)
-        def _():
-            for r in BOTH:
-                for h in range(PARTS):
-                    send_sum(col, r, h).wait_send()
-        return carry
-    lax.fori_loop(0, 4, drain_columns, 0)
-    for h in BOTH:
-        give(h).wait_send()
 
 
 def write_out(*refs):
@@ -826,7 +827,7 @@
                 *stream_sems,
                 *stream_sems, dma((2, 4)), *[dma((4,))] * 3,
                 *[dma((CHIPS, 4))] * 4,
-                dma, dma(pair), dma((3, 2, PARTS)), dma((2, 4, 2, PARTS)), dma(pair), dma(pair),
+                dma, dma(pair), dma((3, 2, PARTS)), dma((2, 4, 2, PARTS)), dma((PARTS,)), dma((PARTS,)),
                 dma((5,)), dma((4,)), dma(pair), dma((4,)), dma((3,)), dma(pair),
             ],
             compiler_params=pltpu.CompilerParams(

time: 307 us -> 301 us (0.980)
  Pallas kernels: 305 us -> 298 us
    pallas_call x1, Pallas kernels: 298 us -> 291 us  [local_backward(): pl.pallas_call(kernel, out_shape=[pltpu.VMEM((own, hidden), BF16), pltpu....]
where the time goes in v7:
time: 301 us; the launch traced here: 299 us
  Pallas kernels  298 us (99%)
    pallas_call x1, Pallas kernels, local_backward(): pl.pallas_call(kernel, out_shape=[pltpu.VMEM((own, hidden), BF16), pltpu....  291 us
    pallas_call x1, Pallas kernels, local_backward(): pl.pallas_call(write_out, out_shape=[shape(a.shape, a.dtype) for a in res...  6.96 us

profile of v7, /device:TPU:0, one launch (start us, length us, event | category | flops | bytes accessed | tf_op | source)
XLA Modules:
  0.0 299.1 jit_solution(12208550341522278847)
XLA Ops:
  0.6 291.4 %mlp_backward.1 = (bf16[256,2048]{1,0:T(8,128)(2,1)S(1)}, bf16[4096,128]{1,0:T(8,128)(2,1)S(1)}, f32[688,2048]{1,0:T(8,128)S(1)}, f32[688,2048]{1,0:T(8,128)S(1)...) custom-call(bf16[256,2048]{1,0:T(8,128)(2,1)} %x.1, ...), custom_call_target="tpu_custom_call" | custom-call | tf_op jit(solution)/shard_map/mlp_backward/pallas_call | solution.py:805
  292.0 7.0 %write_out.1 = (bf16[256,2048]{1,0:T(8,128)(2,1)}, bf16[4096,128]{1,0:T(8,128)(2,1)}, f32[688,2048]{1,0:T(8,128)}, f32[688,2048]{1,0:T(8,128)}, f32[688,2048]{1,0:T(8,128)}, /*index=5*/f32[128,2048]{1,0:T(8,128)}) custom-call(bf16[256,2048]{1,0:T(8,128)(2,1)S(1)} %get-tuple-element.18.refs_0_, bf16[4096,128]{1,0:T(8,128)(2,1)S(1)} %get-tuple-element.19.refs_1_, ...), custom_call_target="tpu_custom_call" | custom-call | tf_op jit(solution)/shard_map/write_out/pallas_call | solution.py:838

commit v8 on v7

--- a/solution.py
+++ b/solution.py
@@ -490,11 +490,6 @@
         return carry
 
     lax.fori_loop(0, 4, hidden_pair, 0)
-    finish(LAST)
-    for copy in keep(LAST):
-        copy.wait()
-    swap(LAST).wait_send()
-
     def carry_on(k, m):
         r, h = 1 - m // PARTS, part_of(m % PARTS)
         col = column(k)
@@ -505,6 +500,15 @@
         mine[...] = (mine[...].astype(F32) + stage[slot].astype(F32)).astype(BF16)
         send_sum(k, r, h).start()
 
+    @pl.when(inner)
+    def _():
+        carry_on(2, 0)
+        carry_on(2, 1)
+    finish(LAST)
+    for copy in keep(LAST):
+        copy.wait()
+    swap(LAST).wait_send()
+
     def settle_part(side, r, h, slot):
         take_sum(side, z, r, h, slot).wait()
         at = tile_at(h, PART)
@@ -560,10 +564,10 @@
         lax.fori_loop(0, hidden // WIDE, tile, 0)
 
     def late_step(i, carry):
-        @pl.when(inner & (i < 2))
-        def _():
-            carry_on(2, 2 * i)
-            carry_on(2, 2 * i + 1)
+        @pl.when(inner & (i == 1))
+        def _():
+            carry_on(2, 2)
+            carry_on(2, 3)
 
         @pl.when(inner & (i > 1))
         def _():

time: 301 us -> 299 us (level)
  no operation moved by 1% of the time
where the time goes in v8:
time: 299 us; the launch traced here: 297 us
  Pallas kernels  296 us (99%)
    pallas_call x1, Pallas kernels, local_backward(): pl.pallas_call(kernel, out_shape=[pltpu.VMEM((own, hidden), BF16), pltpu....  289 us
    pallas_call x1, Pallas kernels, local_backward(): pl.pallas_call(write_out, out_shape=[shape(a.shape, a.dtype) for a in res...  6.96 us

profile of v8, /device:TPU:0, one launch (start us, length us, event | category | flops | bytes accessed | tf_op | source)
XLA Modules:
  0.0 296.6 jit_solution(14324286988464435914)
XLA Ops:
  0.6 288.8 %mlp_backward.1 = (bf16[256,2048]{1,0:T(8,128)(2,1)S(1)}, bf16[4096,128]{1,0:T(8,128)(2,1)S(1)}, f32[688,2048]{1,0:T(8,128)S(1)}, f32[688,2048]{1,0:T(8,128)S(1)...) custom-call(bf16[256,2048]{1,0:T(8,128)(2,1)} %x.1, ...), custom_call_target="tpu_custom_call" | custom-call | tf_op jit(solution)/shard_map/mlp_backward/pallas_call | solution.py:809
  289.4 7.0 %write_out.1 = (bf16[256,2048]{1,0:T(8,128)(2,1)}, bf16[4096,128]{1,0:T(8,128)(2,1)}, f32[688,2048]{1,0:T(8,128)}, f32[688,2048]{1,0:T(8,128)}, f32[688,2048]{1,0:T(8,128)}, /*index=5*/f32[128,2048]{1,0:T(8,128)}) custom-call(bf16[256,2048]{1,0:T(8,128)(2,1)S(1)} %get-tuple-element.18.refs_0_, bf16[4096,128]{1,0:T(8,128)(2,1)S(1)} %get-tuple-element.19.refs_1_, ...), custom_call_target="tpu_custom_call" | custom-call | tf_op jit(solution)/shard_map/write_out/pallas_call | solution.py:842
